TPU v7x, 128 devices: a whole 4x4x4 slice. The times are simulated.
128 devices in a mesh: head: 16 (over z_lo, y, core), row: 8 (over z_hi, x).
Axes of the slice: x: 4, y: 4, z: 4 (z_hi: 2, z_lo: 2; z = z_hi * 2 + z_lo), core: 2. Of those that a mesh axis runs over, the one named last changes fastest.
Arguments:
- token_ids: int32 [2048], replicated, may hold values from 0 to 151643, as said below
- teacher_hidden: bfloat16 [2048, 8192], P('head', 'row'), may hold values from -20 to 20
- teacher_query: bfloat16 [8192, 8192], P('row', 'head'), may hold values from -0.0625 to 0.0625
- teacher_kv: bfloat16 [8192, 2, 1024], P('row', None, 'head'), may hold values from -0.0625 to 0.0625
- student_hidden: bfloat16 [2048, 3584], P('head', 'row'), may hold values from -20 to 20
- student_query: bfloat16 [3584, 3584], P('row', 'head'), may hold values from -0.09375 to 0.09375
- student_kv: bfloat16 [3584, 2, 512], P('row', None, 'head'), may hold values from -0.09375 to 0.09375
Outputs:
- relation_loss: float32 [], replicated
- query_grad: float32 [3584, 3584], P('row', 'head')
- kv_grad: float32 [3584, 2, 512], P('row', None, 'head')
- hidden_grad: float32 [2048, 3584], P('head', 'row')
Inputs may be any that keep to these rules, and one draw needn't show every extreme that they name: `token_ids`: from some position in the second half of the sequence on, if any, every position holds the padding id 151643; before it every id is below 151643.
All inputs are finite; a program needn't handle non-finite values.
Results may differ from a plain program's by a relative error of at most 0.0035.
The roundings to bfloat16 on the way count: a program that leaves them out, or rounds other values in their place, can miss the bound.
Values may be sent and summed in bfloat16 or wider, within the bound.
A program may use at most 192 MiB of HBM per device.

v0:
```python
import functools

import jax
import jax.numpy as jnp
from jax import lax
from jax.sharding import Mesh
from jax.sharding import PartitionSpec as P

HEADS = 64
HEAD = ("head_0", "head_1", "head_2")
ROW = ("row_0", "row_1")
HEAD_ROW = ("head_0", "head_1", "head_2", "row_0", "row_1")


pad_token = 151643
neg_fill = -1e30


def side_by_side(arrays, axis, dim, along):
    ends, at = ([], 0)
    for a in arrays[:-1]:
        at += a.shape[along]
        ends.append(at)
    both = jnp.concatenate(arrays, axis=along)
    return tuple(jnp.split(lax.all_gather(both, axis, axis=dim, tiled=True), ends, axis=along))


def in_blocks(value, dim, count):
    before, after = (value.shape[:dim], value.shape[dim + 1 :])
    return jnp.moveaxis(value.reshape(*before, count, -1, *after), dim, 0)


def sent_and_summed(value, axis, dim):
    blocks = in_blocks(value, dim, lax.axis_size(axis))
    arrived = lax.all_to_all(blocks, axis, split_axis=0, concat_axis=0, tiled=True)
    return arrived.sum(axis=0)


def joined_along(blocks, dim):
    dims = list(blocks.shape[1:])
    dims[dim] *= blocks.shape[0]
    return jnp.moveaxis(blocks, 0, dim).reshape(dims)


def copy_for_each(value, axis):
    count = lax.axis_size(axis)
    return lax.all_to_all(
        jnp.broadcast_to(value[None], (count, *value.shape)), axis, 0, 0, tiled=True
    )


def collect(value, axis, dim):
    return joined_along(copy_for_each(value, axis), dim)


def by_axis(value, axes):
    return functools.reduce(lax.psum, axes, value)


def per_device(
    token_ids, teacher_hidden, teacher_query, teacher_kv, student_hidden, student_query, student_kv
):
    seq_len = token_ids.shape[0]
    local_heads = HEADS // lax.axis_size(HEAD)
    row_count = seq_len // lax.axis_size(ROW)
    row_start = lax.axis_index(ROW) * row_count
    valid_mask = token_ids != pad_token
    key_valid = valid_mask.astype(jnp.float32)
    row_valid = lax.dynamic_slice_in_dim(key_valid, row_start, row_count, 0)
    teacher_feats, student_feats = side_by_side((teacher_hidden, student_hidden), HEAD, 0, 1)
    teacher_weight = jnp.concatenate(
        [teacher_query, teacher_kv.reshape(teacher_kv.shape[0], -1)], axis=1
    )
    student_weight = jnp.concatenate(
        [student_query, student_kv.reshape(student_kv.shape[0], -1)], axis=1
    )
    teacher_qcols = teacher_query.shape[1]
    teacher_kvcols = teacher_kv.shape[2]
    student_qcols = student_query.shape[1]
    student_kvcols = student_kv.shape[2]
    teacher_width = teacher_qcols + 2 * teacher_kvcols
    kinds = [
        (0, teacher_qcols, teacher_width, student_qcols),
        (teacher_qcols, teacher_kvcols, teacher_width + student_qcols, student_kvcols),
        (
            teacher_qcols + teacher_kvcols,
            teacher_kvcols,
            teacher_width + student_qcols + student_kvcols,
            student_kvcols,
        ),
    ]
    teacher_part = jnp.dot(teacher_feats, teacher_weight, preferred_element_type=jnp.float32)
    student_part = jnp.dot(student_feats, student_weight, preferred_element_type=jnp.float32)
    all_rows = lax.psum(jnp.concatenate([teacher_part, student_part], axis=1), ROW).astype(
        jnp.bfloat16
    )
    own_rows = lax.dynamic_slice_in_dim(all_rows, row_start, row_count, 0)
    loss_sum = jnp.zeros((), jnp.float32)
    weight_list = []
    query_list = []
    student_owned = []
    scale_list = []
    for teacher_lo, teacher_cols, student_lo, student_cols in kinds:
        teacher_dim = teacher_cols // local_heads
        student_dim = student_cols // local_heads
        teacher_scale = teacher_dim ** (-0.5)
        student_scale = student_dim ** (-0.5)
        teacher_keys = all_rows[:, teacher_lo : teacher_lo + teacher_cols].reshape(
            seq_len, local_heads, teacher_dim
        )
        teacher_mine = own_rows[:, teacher_lo : teacher_lo + teacher_cols].reshape(
            row_count, local_heads, teacher_dim
        )
        student_keys = all_rows[:, student_lo : student_lo + student_cols].reshape(
            seq_len, local_heads, student_dim
        )
        student_mine = own_rows[:, student_lo : student_lo + student_cols].reshape(
            row_count, local_heads, student_dim
        )
        teacher_logits = (
            jnp.einsum(
                "ihd,jhd->hij", teacher_mine, teacher_keys, preferred_element_type=jnp.float32
            )
            * teacher_scale
        )
        teacher_logits = jnp.where(valid_mask[None, None, :], teacher_logits, neg_fill)
        teacher_log = jax.nn.log_softmax(teacher_logits, axis=-1)
        student_logits = (
            jnp.einsum(
                "ihd,jhd->hij", student_mine, student_keys, preferred_element_type=jnp.float32
            )
            * student_scale
        )
        student_logits = jnp.where(valid_mask[None, None, :], student_logits, neg_fill)
        student_log = jax.nn.log_softmax(student_logits, axis=-1)
        teacher_prob = jnp.exp(teacher_log)
        student_prob = jnp.exp(student_log)
        row_kl = jnp.sum(teacher_prob * (teacher_log - student_log), axis=-1)
        loss_sum = loss_sum + jnp.sum(row_kl * row_valid[None, :])
        weights = ((student_prob - teacher_prob) * row_valid[None, :, None]).astype(jnp.bfloat16)
        query_part = (
            jnp.einsum("hij,jhd->ihd", weights, student_keys, preferred_element_type=jnp.float32)
            * student_scale
        )
        weight_list.append(weights)
        query_list.append(query_part.reshape(row_count, student_cols))
        student_owned.append(student_mine)
        scale_list.append(student_scale)
    query_grads = jnp.concatenate(query_list, axis=1)
    pieces = []
    for kind in range(3):
        sliced = weight_list[kind]
        key_term = (
            jnp.einsum(
                "hij,ihd->jhd", sliced, student_owned[kind], preferred_element_type=jnp.float32
            )
            * scale_list[kind]
        )
        pieces.append(key_term.reshape(row_count * lax.axis_size(ROW), kinds[kind][3]))
    grad_own = (sent_and_summed(jnp.concatenate(pieces, axis=1), ROW, 0) + query_grads).astype(
        jnp.bfloat16
    )
    grad_all = collect(grad_own, ROW, 0)
    weight_grad = lax.dot_general(
        student_feats, grad_all, (((0,), (0,)), ((), ())), preferred_element_type=jnp.float32
    )
    query_out = weight_grad[:, :student_qcols]
    kv_out = weight_grad[:, student_qcols:].reshape(student_kv.shape)
    input_grad = lax.psum_scatter(
        lax.dot_general(
            grad_all, student_weight, (((1,), (1,)), ((), ())), preferred_element_type=jnp.float32
        ),
        HEAD,
        scatter_dimension=0,
        tiled=True,
    )
    kl_sum = by_axis(loss_sum, HEAD_ROW)
    mean_kl = kl_sum / (3.0 * HEADS * jnp.sum(key_valid))
    return (mean_kl, query_out, kv_out, input_grad)


def solution(mesh):
    finer = Mesh(
        mesh.devices.reshape(2, 4, 2, 2, 4), ("head_0", "head_1", "head_2", "row_0", "row_1")
    )
    in_specs = (
        P(),
        P(HEAD, ROW),
        P(ROW, HEAD),
        P(ROW, None, HEAD),
        P(HEAD, ROW),
        P(ROW, HEAD),
        P(ROW, None, HEAD),
    )
    out_specs = (P(), P(ROW, HEAD), P(ROW, None, HEAD), P(HEAD, ROW))
    return jax.shard_map(
        per_device, mesh=finer, in_specs=in_specs, out_specs=out_specs, check_vma=False
    )
```

profile of v0, /device:TPU:1, one launch (start us, length us, event | category | flops | bytes accessed | tf_op | source)
XLA Modules:
  0.0 486.4 jit_solution(6590540234876354017)
XLA Ops:
  13.5 42.8 %all-gather.2.cloned.1.call-done = bf16[2048,1472]{1,0:T(8,128)(2,1)} async-done(((bf16[128,1472]{1,0:T(8,128)(2,1)}), bf16[2048,1472]{1,0:T(8,128)(2,1)}) %all-gather.2.cloned.1.call-update) | async-done | bytes 6029328 | tf_op jit(solution)/shard_map/all_gather | solution.py:25
  58.8 5.1 %fusion.42 = f32[2048,640]{0,1:T(8,128)S(1)} fusion(bf16[2048,1472]{1,0:T(8,128)(2,1)} %all-gather.2.cloned.1.call-done, bf16[1024,128]{1,0:T(8,128)(2,1)S(1)} %copy.38, bf16[1024,512]{1,0:T(8,128)(2,1)} %param.10), kind=kOutput, calls=%fused_computation.55 | convolution fusion | flops 2686976000 | bytes 10747904 | tf_op jit(solution)/shard_map/dot_general | solution.py:92
  63.9 3.9 pad_maximum_fusion
  67.8 158.5 %all-reduce.1 = bf16[2048,928]{0,1:T(8,128)(2,1)} all-reduce(f32[2048,928]{0,1:T(8,128)} %pad_maximum_fusion), channel_id=1, replica_groups=mesh['head_0'=2,'head_1'=4,'head_2'=2,'row_0'=2,'row_1'=4] {'row_0','row..., use_global_device_ids=true, to_apply=%region_0.0 | all-reduce | flops 1900544 | bytes 11403264 | tf_op jit(solution)/shard_map/psum | solution.py:94
  233.7 6.5 %fusion.19 = f32[4,256,2048]{2,1,0:T(8,128)} fusion(pred[2048]{0:T(1024)(128)(4,1)S(1)} %get-tuple-element.25, bf16[256,4,128]{0,2,1:T(8,128)(2,1)} %bitcast.115, bf16[2048,4,128]{0,2,1:T(8,128)(2,1)S(1)} %bitcast.107), kind=kOutput, calls=%fused_computation.44 | convolution fusion | flops 543165440 | bytes 10749952 | tf_op jit(solution)/shard_map/jit(log_softmax)/sub | solution.py:127
  240.2 10.8 %log_subtract_fusion.5 = f32[4,256,2048]{2,1,0:T(8,128)} fusion(f32[4,256,2048]{2,1,0:T(8,128)} %fusion.19), kind=kOutput, calls=%fused_computation.17 | output fusion | flops 2100223 | bytes 16777216 | tf_op jit(solution)/shard_map/jit(log_softmax)/reduce_sum | solution.py:127
  251.7 5.2 %fusion.27 = f32[4,256,2048]{2,1,0:T(8,128)} fusion(pred[2048]{0:T(1024)(128)(4,1)S(1)} %get-tuple-element.25, bf16[256,4,16]{0,2,1:T(8,128)(2,1)S(1)} %bitcast.122, bf16[2048,4,16]{0,2,1:T(8,128)(2,1)S(1)} %bitcast.118), kind=kOutput, calls=%fused_computation.52 | convolution fusion | flops 73403392 | bytes 8685568 | tf_op jit(solution)/shard_map/jit(log_softmax)/sub | solution.py:127
  256.9 10.7 %log_subtract_fusion.1 = f32[4,256,2048]{2,1,0:T(8,128)} fusion(f32[4,256,2048]{2,1,0:T(8,128)} %fusion.27), kind=kOutput, calls=%fused_computation.13 | output fusion | flops 2100223 | bytes 16777216 | tf_op jit(solution)/shard_map/jit(log_softmax)/reduce_sum | solution.py:127
  267.6 5.2 %fusion.23 = f32[4,256,2048]{2,1,0:T(8,128)} fusion(pred[2048]{0:T(1024)(128)(4,1)S(1)} %get-tuple-element.25, bf16[256,4,16]{0,2,1:T(8,128)(2,1)S(1)} %bitcast.121, bf16[2048,4,16]{0,2,1:T(8,128)(2,1)S(1)} %bitcast.117), kind=kOutput, calls=%fused_computation.48 | convolution fusion | flops 73403392 | bytes 8685568 | tf_op jit(solution)/shard_map/jit(log_softmax)/sub | solution.py:127
  272.8 10.7 %log_subtract_fusion.3 = f32[4,256,2048]{2,1,0:T(8,128)} fusion(f32[4,256,2048]{2,1,0:T(8,128)} %fusion.23), kind=kOutput, calls=%fused_computation.15 | output fusion | flops 2100223 | bytes 16777216 | tf_op jit(solution)/shard_map/jit(log_softmax)/reduce_sum | solution.py:127
  283.5 6.6 %fusion.25 = f32[4,256,2048]{2,1,0:T(8,128)} fusion(pred[2048]{0:T(1024)(128)(4,1)S(1)} %get-tuple-element.25, bf16[2048,928]{0,1:T(8,128)(2,1)} %all-reduce.1, s32[]{:T(128)S(6)} %select_n.23, s32[]{:T(128)S(6)} %add.41), kind=kOutput, calls=%fused_computation.50 | convolution fusion | flops 39848960 | bytes 8538120 | tf_op jit(solution)/shard_map/jit(log_softmax)/sub | solution.py:135
  290.1 10.7 %log_subtract_fusion.2 = f32[4,256,2048]{2,1,0:T(8,128)} fusion(f32[4,256,2048]{2,1,0:T(8,128)} %fusion.25), kind=kOutput, calls=%fused_computation.14 | output fusion | flops 2100223 | bytes 16777216 | tf_op jit(solution)/shard_map/jit(log_softmax)/reduce_sum | solution.py:135
  300.8 6.4 %fusion.29 = f32[4,256,2048]{2,1,0:T(8,128)} fusion(pred[2048]{0:T(1024)(128)(4,1)S(1)} %get-tuple-element.25, bf16[2048,928]{0,1:T(8,128)(2,1)} %all-reduce.1, s32[]{:T(128)S(6)} %select_n.23, s32[]{:T(128)S(6)} %add.43), kind=kOutput, calls=%fused_computation.54 | convolution fusion | flops 39848960 | bytes 8538120 | tf_op jit(solution)/shard_map/jit(log_softmax)/sub | solution.py:135
  307.1 10.7 %log_subtract_fusion = f32[4,256,2048]{2,1,0:T(8,128)} fusion(f32[4,256,2048]{2,1,0:T(8,128)} %fusion.29), kind=kOutput, calls=%fused_computation.12 | output fusion | flops 2100223 | bytes 16777216 | tf_op jit(solution)/shard_map/jit(log_softmax)/reduce_sum | solution.py:135
  317.8 5.4 %fusion.21 = f32[4,256,2048]{2,1,0:T(8,128)} fusion(pred[2048]{0:T(1024)(128)(4,1)S(1)} %get-tuple-element.25, bf16[256,4,56]{0,2,1:T(8,128)(2,1)S(1)} %bitcast.113, bf16[2048,4,56]{0,2,1:T(8,128)(2,1)S(1)} %bitcast.105), kind=kOutput, calls=%fused_computation.46 | convolution fusion | flops 241175552 | bytes 9422848 | tf_op jit(solution)/shard_map/jit(log_softmax)/sub | solution.py:135
  323.2 26.7 %multiply_convert_fusion.2 = (bf16[4,256,2048]{2,1,0:T(8,128)(2,1)S(1)}, f32[4,256]{1,0:T(4,128)S(1)}, f32[4,256]{1,0:T(4,128)S(1)}, bf16[4,256,2048]{2,1,0:T(8,...) fusion(f32[4,256,2048]{2,1,0:T(8,128)} %log_subtract_fusion.5, f32[256]{0:T(256)S(1)} %dynamic_slice.7, ...), kind=kOutput, calls=%fused_computation.32 | output fusion | flops 39845888 | bytes 62927872 | tf_op jit(solution)/shard_map/jit(log_softmax)/reduce_sum | solution.py:135
  370.3 22.1 %all-to-all-done = f32[8,256,288]{1,2,0:T(8,128)S(1)} async-done(((f32[8,256,288]{1,2,0:T(8,128)}), f32[8,256,288]{1,2,0:T(8,128)S(1)}, u32[]{:S(2)}, u32[]{:S(2)}) %all-to-all-start) | async-done | bytes 2359328 | tf_op jit(solution)/shard_map/all_to_all | solution.py:35
  393.7 18.0 %all_to_all.10 = bf16[8,256,288]{1,2,0:T(8,128)(2,1)S(1)} all-to-all(bf16[8,256,288]{1,2,0:T(8,128)(2,1)S(1)} %broadcast_in_dim.54), channel_id=1, replica_groups=mesh['head_0'=2,'head_1'=4,'head_2'=2,'row_0'=2,'row_1'=4] {'row_0','row..., dimensions={0} | all-to-all | bytes 2359296 | tf_op jit(solution)/shard_map/all_to_all | solution.py:47
  417.3 4.3 psum.43
  421.6 9.2 %psum.44 = f32[]{:T(128)} all-reduce(f32[]{:T(128)} %psum.43), channel_id=1, replica_groups=mesh['head_0'=2,'head_1'=4,'head_2'=2,'row_0'=2,'row_1'=4] {'head_1'}, use_global_device_ids=true, to_apply=%region_10.12 | all-reduce | flops 1 | bytes 8 | tf_op jit(solution)/shard_map/psum | solution.py:57
  430.8 9.5 %psum.45 = f32[]{:T(128)} all-reduce(f32[]{:T(128)} %psum.44), channel_id=1, replica_groups=mesh['head_0'=2,'head_1'=4,'head_2'=2,'row_0'=2,'row_1'=4] {'head_2'}, use_global_device_ids=true, to_apply=%region_11.13 | all-reduce | flops 1 | bytes 8 | tf_op jit(solution)/shard_map/psum | solution.py:57
  440.2 6.3 %psum.46 = f32[]{:T(128)} all-reduce(f32[]{:T(128)} %psum.45), channel_id=1, replica_groups=mesh['head_0'=2,'head_1'=4,'head_2'=2,'row_0'=2,'row_1'=4] {'row_0'}, use_global_device_ids=true, to_apply=%region_12.14 | all-reduce | flops 1 | bytes 8 | tf_op jit(solution)/shard_map/psum | solution.py:57
  447.2 8.0 %psum.47 = f32[]{:T(128)} all-reduce(f32[]{:T(128)} %psum.46), channel_id=1, replica_groups=mesh['head_0'=2,'head_1'=4,'head_2'=2,'row_0'=2,'row_1'=4] {'row_1'}, use_global_device_ids=true, to_apply=%region_13.15 | all-reduce | flops 1 | bytes 8 | tf_op jit(solution)/shard_map/psum | solution.py:57
  459.9 18.1 %reduce-scatter.2.cloned.1.call-done = f32[128,448]{0,1:T(8,128)} async-done(((f32[2048,448]{0,1:T(8,128)}), f32[128,448]{0,1:T(8,128)}) %reduce-scatter.2.cloned.1.call-update) | async-done | bytes 229392 | tf_op jit(solution)/shard_map/reduce_scatter | solution.py:169
  (56 shorter events, 46.2 us)
Async XLA Ops:
  7.2 49.1 %all-gather.2.cloned.1.call-start = ((), (), s32[]{:S(2)}) async-start(), calls=%async_computation.3 | async-start | bytes 6684672 | tf_op jit(solution)/shard_map/all_gather | solution.py:25
  240.2 11.5 %copy-start.6 = (bf16[2048,64]{0,1:T(8,128)(2,1)S(1)}, bf16[2048,64]{0,1:T(8,128)(2,1)}, u32[]{:S(2)}) copy-start(bf16[2048,64]{0,1:T(8,128)(2,1)} %get-tuple-element.33) | copy-start | bytes 786436
  256.9 10.7 %copy-start.5 = (bf16[2048,64]{0,1:T(8,128)(2,1)S(1)}, bf16[2048,64]{0,1:T(8,128)(2,1)}, u32[]{:S(2)}) copy-start(bf16[2048,64]{0,1:T(8,128)(2,1)} %get-tuple-element.32) | copy-start | bytes 786436
  349.9 4.1 copy-start
  349.9 4.1 copy-start.2
  349.9 4.5 copy-start.3
  357.5 35.0 %all-to-all-start = ((f32[8,256,288]{1,2,0:T(8,128)}), f32[8,256,288]{1,2,0:T(8,128)S(1)}, u32[]{:S(2)}, u32[]{:S(2)}) async-start(f32[8,256,288]{1,2,0:T(8,128)} %pad_maximum_fusion.1), calls=%async_computation | async-start | bytes 4718592 | tf_op jit(solution)/shard_map/all_to_all | solution.py:35
  361.1 116.9 %reduce-scatter.2.cloned.1.call-start = ((), (), s32[]{:S(2)}) async-start(), calls=%async_computation.4 | async-start | bytes 3899392 | tf_op jit(solution)/shard_map/reduce_scatter | solution.py:169
  361.1 7.1 %copy-start.1 = (bf16[4,256,2048]{2,1,0:T(8,128)(2,1)S(1)}, bf16[4,256,2048]{2,1,0:T(8,128)(2,1)}, u32[]{:S(2)}) copy-start(bf16[4,256,2048]{2,1,0:T(8,128)(2,1)} %copy-done) | copy-start | bytes 12582916
  370.3 41.5 %copy-start.4 = (bf16[448,224]{1,0:T(8,128)(2,1)S(1)}, bf16[448,224]{1,0:T(8,128)(2,1)}, u32[]{:S(2)}) copy-start(bf16[448,224]{1,0:T(8,128)(2,1)} %param.13) | copy-start | bytes 602116
Sparse Core Ops, SparseCore 0:
  10.2 46.0 all-gather.1
  414.9 63.0 reduce-scatter.1
where the time goes:
time: 494 us; the launch traced here: 486 us
  blocking collectives  214 us (43%)
  other arithmetic  90.6 us (18%)
  waiting for transfers between devices  83.1 us (17%)
  matrix products  60.8 us (12%)
  between operations  19 us (4%)
  local copies, waits for them, and re-layouts  15.4 us (3%)
    psum x1, blocking collectives, per_device(): lax.psum(jnp.concatenate([teacher_part, student_part], axis=1), ROW)  159 us
    reduce_sum x3, other arithmetic, per_device(): student_log = jax.nn.log_softmax(student_logits, axis=-1)  48 us
    all_gather x1, waiting for transfers between devices, side_by_side(): lax.all_gather(both, axis, axis=dim, tiled=True)  42.8 us
    psum x5, blocking collectives, by_axis(): return functools.reduce(lax.psum, axes, value)  37.3 us
    reduce_sum x3, other arithmetic, per_device(): teacher_log = jax.nn.log_softmax(teacher_logits, axis=-1)  32.2 us
    all_to_all x1, waiting for transfers between devices, sent_and_summed(): lax.all_to_all(blocks, axis, split_axis=0, concat_axis=0, tiled=True)  22.1 us
    sub x3, matrix products, per_device(): student_log = jax.nn.log_softmax(student_logits, axis=-1)  18.4 us
    reduce_scatter x1, waiting for transfers between devices, per_device(): lax.psum_scatter(lax.dot_general(grad_all, student_weight, (((1,), (1,)),...  18.1 us
  transfers between devices with their start and end apart: 3, of which 3 were waited for; matrix products, arithmetic and copies ran while one was open for 4% of the time, Pallas kernels for 0%

commit v1 on v0

v1 whole, which is shorter than its diff:
```python
import functools
import math

import jax
import jax.numpy as jnp
from jax import lax
from jax.experimental import pallas as pl
from jax.experimental.pallas import tpu as pltpu
from jax.sharding import Mesh
from jax.sharding import PartitionSpec as P

HEADS = 64
HEAD = ("head_0", "head_1", "head_2")
ROW = ("row_0", "row_1")

pad_token = 151643
neg_fill = -1e30
LOG2E = math.log2(math.e)
LN2 = math.log(2.0)

TILE = 256
GROUP = 32
LANES = 128


def relation_kernel(tdims, sdims, n_ref, p_ref, *refs):
    kinds = len(tdims)
    town, sown = refs[:kinds], refs[kinds : 2 * kinds]
    tall, sall = refs[2 * kinds : 3 * kinds], refs[3 * kinds : 4 * kinds]
    qp_ref, kp_ref, loss_ref, dt_ref, ds_ref, mt_ref, ms_ref, w_ref = refs[4 * kinds :]
    seq = tall[0].shape[1]
    step = pl.program_id(0)
    count = n_ref[0]
    first_row = (2 * step + p_ref[0]) * TILE

    @pl.when(step == 0)
    def _():
        kp_ref[...] = jnp.zeros_like(kp_ref)
        loss_ref[...] = jnp.zeros_like(loss_ref)

    @pl.when(first_row >= count)
    def _():
        qp_ref[...] = jnp.zeros_like(qp_ref)

    @pl.when(first_row < count)
    def _():
        at = 0
        for kind in range(kinds):
            scale_t = LOG2E * tdims[kind] ** (-0.5)
            scale_s = LOG2E * sdims[kind] ** (-0.5)
            for own, every, d_ref, m_ref in (
                (town[kind], tall[kind], dt_ref, mt_ref),
                (sown[kind], sall[kind], ds_ref, ms_ref),
            ):
                left = own[...]
                top = jnp.full((TILE, LANES), -jnp.inf, jnp.float32)
                for c in range(0, seq, TILE):
                    d = lax.dot_general(
                        left,
                        every[:, c : c + TILE],
                        (((0,), (0,)), ((), ())),
                        preferred_element_type=jnp.float32,
                    )
                    d_ref[:, c : c + TILE] = d
                    for k in range(0, TILE, LANES):
                        top = jnp.maximum(top, d[:, k : k + LANES])
                m_ref[...] = jnp.broadcast_to(
                    jnp.max(top, axis=1, keepdims=True), (TILE, LANES)
                )

            def group(g, loss):
                rows = pl.ds(pl.multiple_of(g * GROUP, GROUP), GROUP)
                mt, ms = mt_ref[rows, :], ms_ref[rows, :]
                zt = jnp.zeros((GROUP, LANES), jnp.float32)
                zs = jnp.zeros((GROUP, LANES), jnp.float32)
                kl = jnp.zeros((GROUP, LANES), jnp.float32)
                for c in range(0, seq, LANES):
                    xt = (dt_ref[rows, c : c + LANES] - mt) * scale_t
                    xs = (ds_ref[rows, c : c + LANES] - ms) * scale_s
                    et, es = jnp.exp2(xt), jnp.exp2(xs)
                    zt, zs, kl = zt + et, zs + es, kl + et * (xt - xs)
                    dt_ref[rows, c : c + LANES] = et
                    ds_ref[rows, c : c + LANES] = es
                zt = jnp.sum(zt, axis=1, keepdims=True)
                zs = jnp.sum(zs, axis=1, keepdims=True)
                kl = jnp.sum(kl, axis=1, keepdims=True)
                row = first_row + g * GROUP + lax.broadcasted_iota(jnp.int32, (GROUP, 1), 0)
                valid = row < count
                loss = loss + jnp.where(valid, kl / zt * LN2 + jnp.log(zs) - jnp.log(zt), 0.0)
                rt = jnp.broadcast_to(jnp.where(valid, 1.0 / zt, 0.0), (GROUP, LANES))
                rs = jnp.broadcast_to(jnp.where(valid, 1.0 / zs, 0.0), (GROUP, LANES))
                for c in range(0, seq, LANES):
                    w_ref[rows, c : c + LANES] = (
                        ds_ref[rows, c : c + LANES] * rs - dt_ref[rows, c : c + LANES] * rt
                    ).astype(jnp.bfloat16)
                return loss

            loss = lax.fori_loop(
                0, TILE // GROUP, group, jnp.zeros((GROUP, 1), jnp.float32)
            )
            loss_ref[...] += jnp.broadcast_to(loss, loss_ref.shape)
            width = sdims[kind]
            qp_ref[at : at + width, :] = lax.dot_general(
                sall[kind][...],
                w_ref[...],
                (((1,), (1,)), ((), ())),
                preferred_element_type=jnp.float32,
            )[:width]
            left = sown[kind][...]
            for c in range(0, seq, 2 * TILE):
                kp_ref[at : at + width, c : c + 2 * TILE] += lax.dot_general(
                    left,
                    w_ref[:, c : c + 2 * TILE],
                    (((1,), (0,)), ((), ())),
                    preferred_element_type=jnp.float32,
                )[:width]
            at += width


def relations(count, half, tdims, sdims, town, sown, tall, sall):
    seq = tall[0].shape[1]
    mine = town[0].shape[1]
    total = sum(sdims)
    block = lambda a: pl.BlockSpec((a.shape[0], TILE), lambda i: (0, i))
    whole = lambda a: pl.BlockSpec(a.shape, lambda i: (0, 0))
    smem = pl.BlockSpec(memory_space=pltpu.SMEM)
    return pl.pallas_call(
        functools.partial(relation_kernel, tdims, sdims),
        grid=(mine // TILE,),
        in_specs=[smem, smem]
        + [block(a) for a in town + sown]
        + [whole(a) for a in tall + sall],
        out_specs=[
            pl.BlockSpec((total, TILE), lambda i: (0, i)),
            pl.BlockSpec((total, seq), lambda i: (0, 0)),
            pl.BlockSpec((GROUP, LANES), lambda i: (0, 0)),
        ],
        out_shape=[
            jax.ShapeDtypeStruct((total, mine), jnp.float32),
            jax.ShapeDtypeStruct((total, seq), jnp.float32),
            jax.ShapeDtypeStruct((GROUP, LANES), jnp.float32),
        ],
        scratch_shapes=[
            pltpu.VMEM((TILE, seq), jnp.float32),
            pltpu.VMEM((TILE, seq), jnp.float32),
            pltpu.VMEM((TILE, LANES), jnp.float32),
            pltpu.VMEM((TILE, LANES), jnp.float32),
            pltpu.VMEM((TILE, seq), jnp.bfloat16),
        ],
        compiler_params=pltpu.CompilerParams(vmem_limit_bytes=40 * 2**20),
    )(count, half, *town, *sown, *tall, *sall)


def own_tokens(rows, half):
    cut = rows.reshape(rows.shape[0], -1, 2, TILE)
    return lax.dynamic_index_in_dim(cut, half, 2, keepdims=False).reshape(rows.shape[0], -1)


def by_head(query, kv, heads):
    feats = query.shape[0]
    parts = [
        query.reshape(feats, heads, -1),
        kv[:, 0].reshape(feats, heads, -1),
        kv[:, 1].reshape(feats, heads, -1),
    ]
    return jnp.concatenate(parts, axis=2)


def with_mask_row(rows, last):
    count = rows.shape[0]
    pad = -(count + 1) % 16
    return jnp.concatenate(
        [rows, last[None].astype(rows.dtype), jnp.zeros((pad, rows.shape[1]), rows.dtype)]
    )


def pieces(value):
    out = []
    for _ in range(3):
        top = lax.reduce_precision(value, 8, 7)
        out.append(top.astype(jnp.bfloat16))
        value = value - top
    return jnp.stack(out)


def copy_for_each(value, axis):
    size = lax.axis_size(axis)
    return lax.all_to_all(
        jnp.broadcast_to(value[None], (size, *value.shape)), axis, 0, 0, tiled=True
    )


def per_device(
    token_ids, teacher_hidden, teacher_query, teacher_kv, student_hidden, student_query, student_kv
):
    seq_len = token_ids.shape[0]
    local_heads = HEADS // lax.axis_size(HEAD)
    rows = lax.axis_size(ROW)
    me = lax.axis_index(ROW)
    half = me % 2
    valid_mask = token_ids != pad_token
    count = jnp.sum(valid_mask.astype(jnp.int32))

    both = jnp.concatenate([teacher_hidden, student_hidden], axis=1)
    feats = lax.all_gather(both, HEAD, axis=0, tiled=True)
    teacher_feats = feats[:, : teacher_hidden.shape[1]]
    student_feats = feats[:, teacher_hidden.shape[1] :]

    tdims = tuple(
        c // local_heads for c in (teacher_query.shape[1], teacher_kv.shape[2], teacher_kv.shape[2])
    )
    sdims = tuple(
        c // local_heads for c in (student_query.shape[1], student_kv.shape[2], student_kv.shape[2])
    )
    twidth, swidth = sum(tdims), sum(sdims)
    teacher_weight = by_head(teacher_query, teacher_kv, local_heads)
    student_weight = by_head(student_query, student_kv, local_heads)
    student_padded = jnp.pad(student_weight, ((0, 0), (0, 0), (0, -swidth % 16)))
    swidth_pad = student_padded.shape[2]
    project = lambda w, x: lax.dot_general(
        w.reshape(w.shape[0], -1),
        x,
        (((0,), (1,)), ((), ())),
        preferred_element_type=jnp.float32,
    )
    student_part = project(student_padded, student_feats)
    teacher_part = project(teacher_weight, teacher_feats)

    def reduced(part):
        arrived = lax.all_to_all(
            part.reshape(rows, -1, seq_len), ROW, split_axis=0, concat_axis=0, tiled=True
        )
        return arrived.sum(axis=0).astype(jnp.bfloat16)

    own_half = jnp.concatenate([reduced(teacher_part), reduced(student_part)])
    swap = [(i, i ^ 1) for i in range(lax.axis_size(ROW[1]))]
    other = lax.ppermute(own_half, ROW[1], swap)
    low = jnp.where(half == 0, own_half, other)
    high = jnp.where(half == 0, other, own_half)
    tcut = twidth // 2
    teacher_rows = jnp.concatenate([low[:tcut], high[:tcut]])
    student_rows = jnp.concatenate([low[tcut:], high[tcut:]])

    def cut(block, dims):
        out, at = [], 0
        for d in dims:
            out.append(block[at : at + d])
            at += d
        return out

    bias = jnp.where(valid_mask, 0.0, neg_fill)
    ones = jnp.ones((seq_len // 2,), jnp.float32)
    every = lambda parts: [with_mask_row(a, bias) for a in parts]
    mine = lambda parts: [with_mask_row(own_tokens(a, half), ones) for a in parts]
    tparts, sparts = cut(teacher_rows, tdims), cut(student_rows, sdims)
    query_part, key_part, loss = relations(
        count[None],
        half[None].astype(jnp.int32),
        tdims,
        sdims,
        mine(tparts),
        mine(sparts),
        every(tparts),
        every(sparts),
    )
    loss_sum = jnp.sum(loss[:, 0])
    from_other = lax.ppermute(own_tokens(key_part, 1 - half), ROW[1], swap)
    scale = jnp.concatenate([jnp.full((d, 1), d ** (-0.5), jnp.float32) for d in sdims])
    grad_own = ((query_part + own_tokens(key_part, half) + from_other) * scale).astype(jnp.bfloat16)
    below = -swidth % 16
    extra = jnp.zeros((below, grad_own.shape[1]), jnp.bfloat16).at[0, :3].set(pieces(loss_sum))
    arrived = copy_for_each(jnp.concatenate([grad_own, extra]), ROW)
    row_loss = jnp.sum(arrived[:, swidth, :3].astype(jnp.float32))
    grads = (
        arrived[:, :swidth].reshape(local_heads, 2, swidth, -1, TILE)
        .transpose(0, 2, 3, 1, 4)
        .reshape(local_heads * swidth, seq_len)
    )
    weight_grad = lax.dot_general(
        student_feats, grads, (((0,), (1,)), ((), ())), preferred_element_type=jnp.float32
    ).reshape(student_feats.shape[1], local_heads, swidth)
    q, k = sdims[0], sdims[1]
    query_out = weight_grad[:, :, :q].reshape(student_query.shape)
    kv_out = jnp.stack(
        [
            weight_grad[:, :, q : q + k].reshape(-1, local_heads * k),
            weight_grad[:, :, q + k :].reshape(-1, local_heads * k),
        ],
        axis=1,
    )

    heads = lax.axis_size(HEAD)
    all_weight = lax.all_gather(
        student_weight.reshape(student_weight.shape[0], -1).T, HEAD, axis=0, tiled=True
    )
    blocks = jnp.moveaxis(grads.reshape(grads.shape[0], heads, -1), 1, 0)
    extra = jnp.zeros((16, blocks.shape[2]), jnp.bfloat16).at[0, :3].set(pieces(row_loss))
    sent = jnp.concatenate([blocks, jnp.broadcast_to(extra[None], (heads, *extra.shape))], axis=1)
    got = lax.all_to_all(sent, HEAD, split_axis=0, concat_axis=0, tiled=True)
    kl_sum = jnp.sum(got[:, grads.shape[0], :3].astype(jnp.float32))
    input_grad = lax.dot_general(
        got[:, : grads.shape[0]].reshape(heads * grads.shape[0], -1),
        all_weight,
        (((0,), (0,)), ((), ())),
        preferred_element_type=jnp.float32,
    )
    mean_kl = kl_sum / (3.0 * HEADS * count.astype(jnp.float32))
    return (mean_kl, query_out, kv_out, input_grad)


def solution(mesh):
    finer = Mesh(
        mesh.devices.reshape(2, 4, 2, 2, 4), ("head_0", "head_1", "head_2", "row_0", "row_1")
    )
    in_specs = (
        P(),
        P(HEAD, ROW),
        P(ROW, HEAD),
        P(ROW, None, HEAD),
        P(HEAD, ROW),
        P(ROW, HEAD),
        P(ROW, None, HEAD),
    )
    out_specs = (P(), P(ROW, HEAD), P(ROW, None, HEAD), P(HEAD, ROW))
    return jax.shard_map(
        per_device, mesh=finer, in_specs=in_specs, out_specs=out_specs, check_vma=False
    )
```

time: 494 us -> 317 us (0.64); the launches traced: 486 us -> 317 us
  blocking collectives: 214 us -> 24.3 us
  other arithmetic: 90.6 us -> 14.7 us
  waiting for transfers between devices: 83.1 us -> 139 us
  matrix products: 60.8 us -> 19.5 us
  starting transfers between devices: 3.69 us -> 37 us
  Pallas kernels: 0 us -> 26.9 us
  local copies, waits for them, and re-layouts: 15.4 us -> 27.6 us
  between operations: 19 us -> 27.8 us
    psum x6 -> x0, blocking collectives: 196 us -> none  [the longest x1 159 us: per_device(): lax.psum(jnp.concatenate([teacher_part, student_part], axis=1), ROW)]
    reduce_sum x9 -> x6, other arithmetic: 82.3 us -> 5.61 us  [the longest x2 3.15 us: reduced(): return arrived.sum(axis=0).astype(jnp.bfloat16)]
    all_to_all x1 -> x3, waiting for transfers between devices: 22.1 us -> 85.2 us  [the longest x2 74.1 us: reduced(): lax.all_to_all(part.reshape(rows, -1, seq_len), ROW, split_axis=0, concat...]
    sub x6 -> x0, matrix products: 35.2 us -> none  [the longest x3 18.4 us: per_device(): student_log = jax.nn.log_softmax(student_logits, axis=-1)]
    pallas_call x0 -> x1, Pallas kernels: none -> 26.9 us  [relations(): pl.pallas_call(functools.partial(relation_kernel, tdims, sdims), grid=(mi...]
    all_to_all x1 -> x3, starting transfers between devices: 3.61 us -> 24.9 us  [the longest x2 16.1 us: reduced(): lax.all_to_all(part.reshape(rows, -1, seq_len), ROW, split_axis=0, concat...]
    reduce_scatter x1 -> x0, waiting for transfers between devices: 18.1 us -> none  [per_device(): lax.psum_scatter(lax.dot_general(grad_all, student_weight, (((1,), (1,)),...]
    ppermute x0 -> x2, starting transfers between devices: none -> 12 us  [the longest x1 11.9 us: per_device(): other = lax.ppermute(own_half, ROW[1], swap)]
  transfers between devices with their start and end apart: 3 -> 7, of which waited for: 3 -> 5; matrix products, arithmetic and copies ran while one was open for 4% -> 16% of each run, Pallas kernels for 0% -> 9%
where the time goes in v1:
time: 317 us
  waiting for transfers between devices  139 us (44%)
  starting transfers between devices  37 us (12%)
  between operations  27.8 us (9%)
  local copies, waits for them, and re-layouts  27.6 us (9%)
  Pallas kernels  26.9 us (8%)
  blocking collectives  24.3 us (8%)
  matrix products  19.5 us (6%)
  other arithmetic  14.7 us (5%)
    all_to_all x2, waiting for transfers between devices, reduced(): lax.all_to_all(part.reshape(rows, -1, seq_len), ROW, split_axis=0, concat...  74.1 us
    all_gather x1, waiting for transfers between devices, per_device(): feats = lax.all_gather(both, HEAD, axis=0, tiled=True)  44.4 us
    pallas_call x1, Pallas kernels, relations(): pl.pallas_call(functools.partial(relation_kernel, tdims, sdims), grid=(mi...  26.9 us
    all_to_all x1, blocking collectives, copy_for_each(): lax.all_to_all(jnp.broadcast_to(value[None], (size, *value.shape)), axis,...  24.3 us
    all_to_all x2, starting transfers between devices, reduced(): lax.all_to_all(part.reshape(rows, -1, seq_len), ROW, split_axis=0, concat...  16.1 us
    dot_general x2, matrix products, per_device(): lax.dot_general(w.reshape(w.shape[0], -1), x, (((0,), (1,)), ((), ())), p...  12 us
    ppermute x1, starting transfers between devices, per_device(): other = lax.ppermute(own_half, ROW[1], swap)  11.9 us
    all_to_all x1, waiting for transfers between devices, per_device(): got = lax.all_to_all(sent, HEAD, split_axis=0, concat_axis=0, tiled=True)  11.1 us
  transfers between devices with their start and end apart: 7, of which 5 were waited for; matrix products, arithmetic and copies ran while one was open for 16% of the time, Pallas kernels for 9%

profile of v1, /device:TPU:1, one launch (start us, length us, event | category | flops | bytes accessed | tf_op | source)
XLA Modules:
  0.0 316.5 jit_solution(14347359206112913516)
XLA Ops:
  8.2 1.7 pad_maximum_fusion.5
  11.9 44.4 %all-gather.3.cloned.1.call-done = bf16[2048,1472]{1,0:T(8,128)(2,1)} async-done(((bf16[128,1472]{1,0:T(8,128)(2,1)}), bf16[2048,1472]{1,0:T(8,128)(2,1)}) %all-gather.3.cloned.1.call-update) | async-done | bytes 6029328 | tf_op jit(solution)/shard_map/all_gather | solution.py:205
  56.3 4.1 %fusion.2 = f32[8,40,2048]{2,1,0:T(8,128)} fusion(bf16[8,40,448]{2,1,0:T(8,128)(2,1)S(1)} %bitcast.75, bf16[2048,1472]{1,0:T(8,128)(2,1)} %all-gather.3.cloned.1.call-done), kind=kOutput, calls=%fused_computation.5 | convolution fusion | flops 587202560 | bytes 5005312 | tf_op jit(solution)/shard_map/dot_general | solution.py:220
  60.4 6.4 %all-to-all-start.1 = ((f32[8,40,2048]{2,1,0:T(8,128)}), f32[8,40,2048]{2,1,0:T(8,128)S(1)}, u32[]{:S(2)}, u32[]{:S(2)}) async-start(f32[8,40,2048]{2,1,0:T(8,128)} %fusion.2), calls=%async_computation.1 | async-start | bytes 5242880 | tf_op jit(solution)/shard_map/all_to_all | solution.py:230
  69.6 2.1 reshape.155
  71.8 4.5 %pad_maximum_fusion = bf16[1024,4,160]{2,1,0:T(4,128)(2,1)} fusion(bf16[1024,4,16]{2,1,0:T(4,128)(2,1)} %copy.52, bf16[1024,4,16]{2,1,0:T(4,128)(2,1)} %copy.51, bf16[1024,4,128]{2,1,0:T(4,128)(2,1)} %reshape.155), kind=kLoop, calls=%fused_computation.3 | loop fusion | flops 3932160 | bytes 2621440 | tf_op jit(solution)/shard_map/concatenate | solution.py:166
  76.3 4.2 %copy.53 = bf16[1024,4,160]{0,2,1:T(8,128)(2,1)} copy(bf16[1024,4,160]{2,1,0:T(4,128)(2,1)} %pad_maximum_fusion) | data formatting | bytes 2621440 | tf_op jit(solution)/shard_map/concatenate | solution.py:166
  80.5 7.9 %fusion = f32[8,80,2048]{2,1,0:T(8,128)} fusion(bf16[8,80,1024]{2,1,0:T(8,128)(2,1)} %bitcast.76, bf16[2048,1472]{1,0:T(8,128)(2,1)} %all-gather.3.cloned.1.call-done), kind=kOutput, calls=%fused_computation.1 | convolution fusion | flops 2684354560 | bytes 10747904 | tf_op jit(solution)/shard_map/dot_general | solution.py:220
  88.4 12.6 %all-to-all-done.1 = f32[8,40,2048]{2,1,0:T(8,128)S(1)} async-done(((f32[8,40,2048]{2,1,0:T(8,128)}), f32[8,40,2048]{2,1,0:T(8,128)S(1)}, u32[]{:S(2)}, u32[]{:S(2)}) %all-to-all-start.1) | async-done | bytes 2621472 | tf_op jit(solution)/shard_map/all_to_all | solution.py:230
  101.0 9.7 %all-to-all-start = ((f32[8,80,2048]{2,1,0:T(8,128)}), f32[8,80,2048]{2,1,0:T(8,128)}, u32[]{:S(2)}, u32[]{:S(2)}) async-start(f32[8,80,2048]{2,1,0:T(8,128)} %fusion), calls=%async_computation | async-start | bytes 10485760 | tf_op jit(solution)/shard_map/all_to_all | solution.py:230
  111.6 61.5 %all-to-all-done = f32[8,80,2048]{2,1,0:T(8,128)} async-done(((f32[8,80,2048]{2,1,0:T(8,128)}), f32[8,80,2048]{2,1,0:T(8,128)}, u32[]{:S(2)}, u32[]{:S(2)}) %all-to-all-start) | async-done | bytes 5242912 | tf_op jit(solution)/shard_map/all_to_all | solution.py:230
  173.1 3.0 reduce_sum.55
  176.2 11.9 %collective-permute-start = (bf16[120,2048]{1,0:T(8,128)(2,1)S(1)}, bf16[120,2048]{1,0:T(8,128)(2,1)S(1)}, u32[]{:S(2)}, u32[]{:S(2)}) collective-permute-start(bf16[120,2048]{1,0:T(8,128)(2,1)S(1)} %pad_maximum_fusion.4), channel_id=1, source_target_pairs={{0,1},{1,0},{2,3},{3,2},{4,5},{5,4},{6,7},{7,6},{8,9},{9,8},{10,11... | collective-permute-start | bytes 1474568 | tf_op jit(solution)/shard_map/ppermute | solution.py:237
  188.7 8.3 %collective-permute-done = bf16[120,2048]{1,0:T(8,128)(2,1)S(1)} collective-permute-done((bf16[120,2048]{1,0:T(8,128)(2,1)S(1)}, bf16[120,2048]{1,0:T(8,128)(2,1)S(1)}, u32[]{:S(2)}, u32[]{:S(2)}) %collective-permute-start) | collective-permute-done | bytes 491552 | tf_op jit(solution)/shard_map/ppermute | solution.py:237
  200.8 26.9 %shard_map.102 = (f32[72,1024]{1,0:T(8,128)S(1)}, f32[72,2048]{1,0:T(8,128)S(1)}, f32[32,128]{1,0:T(8,128)S(1)}) custom-call(s32[1]{0:T(128)} %bitcast.n_ref, s32[1]{0:T(128)} %bitcast.1.p_ref, bf16[144,1024]{1,0:T(8,128)(2,1)S(1)} %pad_maximum_fusion.7.refs_0_, bf16[32,1024]{1,0:T(8,128)(2,1)S(1)} %get-tuple-element.71.refs_1_, ...), custom_call_target="tpu_custom_call" | custom-call | tf_op jit(solution)/shard_map/pallas_call | solution.py:127
  228.3 1.7 dynamic-slice_reduce_fusion.1
  237.2 24.3 %all_to_all.20 = bf16[8,80,1024]{2,1,0:T(8,128)(2,1)S(1)} all-to-all(bf16[8,80,1024]{2,1,0:T(8,128)(2,1)S(1)} %broadcast_in_dim.42), channel_id=1, replica_groups=mesh['head_0'=2,'head_1'=4,'head_2'=2,'row_0'=2,'row_1'=4] {'row_0','row..., dimensions={0} | all-to-all | bytes 2621440 | tf_op jit(solution)/shard_map/all_to_all | solution.py:188
  267.2 1.7 reshape.175
  269.0 3.1 copy.62
  275.6 8.8 %all-to-all-start.3 = ((bf16[16,304,128]{2,1,0:T(8,128)(2,1)}), bf16[16,304,128]{2,1,0:T(8,128)(2,1)S(1)}, u32[]{:S(2)}, u32[]{:S(2)}) async-start(bf16[16,304,128]{2,1,0:T(8,128)(2,1)} %copy.63), calls=%async_computation.3 | async-start | bytes 2490368 | tf_op jit(solution)/shard_map/all_to_all | solution.py:299
  285.1 1.7 dot_general.28
  286.8 2.7 fusion.1
  291.2 11.1 %all-to-all-done.3 = bf16[16,304,128]{2,1,0:T(8,128)(2,1)S(1)} async-done(((bf16[16,304,128]{2,1,0:T(8,128)(2,1)}), bf16[16,304,128]{2,1,0:T(8,128)(2,1)S(1)}, u32[]{:S(2)}, u32[]{:S(2)}) %all-to-all-start.3) | async-done | bytes 1245216 | tf_op jit(solution)/shard_map/all_to_all | solution.py:299
  303.7 4.9 %fusion.10 = f32[128,448]{0,1:T(8,128)} fusion(bf16[4608,128]{1,0:T(8,128)(2,1)S(1)} %bitcast.72, bf16[4608,448]{1,0:T(8,128)(2,1)} %all-gather.5.cloned.1.call-done), kind=kOutput, calls=%fused_computation.65 | convolution fusion | flops 528482304 | bytes 5537792 | tf_op jit(solution)/shard_map/dot_general | solution.py:301
  (85 shorter events, 19.2 us)
Async XLA Ops:
  7.2 49.1 %all-gather.3.cloned.1.call-start = ((), (), s32[]{:S(2)}) async-start(), calls=%async_computation.4 | async-start | bytes 6684672 | tf_op jit(solution)/shard_map/all_gather | solution.py:205
  11.9 48.5 %copy-start = (bf16[448,4,72]{0,2,1:T(8,128)(2,1)}, bf16[448,4,72]{0,2,1:T(8,128)(2,1)S(1)}, u32[]{:S(2)}) copy-start(bf16[448,4,72]{0,2,1:T(8,128)(2,1)S(1)} %pad_maximum_fusion.6) | copy-start | bytes 774148
  60.4 6.4 %copy-start.1 = (bf16[1024,2,64]{0,2,1:T(8,128)(2,1)S(1)}, bf16[1024,2,64]{0,2,1:T(8,128)(2,1)}, u32[]{:S(2)}) copy-start(bf16[1024,2,64]{0,2,1:T(8,128)(2,1)} %param.14) | copy-start | bytes 786436
  60.4 40.6 %all-to-all-start.1 = ((f32[8,40,2048]{2,1,0:T(8,128)}), f32[8,40,2048]{2,1,0:T(8,128)S(1)}, u32[]{:S(2)}, u32[]{:S(2)}) async-start(f32[8,40,2048]{2,1,0:T(8,128)} %fusion.2), calls=%async_computation.1 | async-start | bytes 5242880 | tf_op jit(solution)/shard_map/all_to_all | solution.py:230
  101.0 72.1 %all-to-all-start = ((f32[8,80,2048]{2,1,0:T(8,128)}), f32[8,80,2048]{2,1,0:T(8,128)}, u32[]{:S(2)}, u32[]{:S(2)}) async-start(f32[8,80,2048]{2,1,0:T(8,128)} %fusion), calls=%async_computation | async-start | bytes 10485760 | tf_op jit(solution)/shard_map/all_to_all | solution.py:230
  110.7 193.0 %all-gather.5.cloned.1.call-start = ((), (), s32[]{:S(2)}) async-start(), calls=%async_computation.5 | async-start | bytes 5013504 | tf_op jit(solution)/shard_map/all_gather | solution.py:293
  111.6 76.5 %copy-start.2 = (s32[2048]{0:T(1024)S(1)}, s32[2048]{0:T(1024)}, u32[]{:S(2)}) copy-start(s32[2048]{0:T(1024)} %param.11) | copy-start | bytes 24580
  176.2 20.9 %collective-permute-start = (bf16[120,2048]{1,0:T(8,128)(2,1)S(1)}, bf16[120,2048]{1,0:T(8,128)(2,1)S(1)}, u32[]{:S(2)}, u32[]{:S(2)}) collective-permute-start(bf16[120,2048]{1,0:T(8,128)(2,1)S(1)} %pad_maximum_fusion.4), channel_id=1, source_target_pairs={{0,1},{1,0},{2,3},{3,2},{4,5},{5,4},{6,7},{7,6},{8,9},{9,8},{10,11... | collective-permute-start | bytes 1474568 | tf_op jit(solution)/shard_map/ppermute | solution.py:237
  227.7 9.2 %copy-start.3 = (f32[72]{0:T(128)S(1)}, f32[72]{0:T(128)}, u32[]{:S(2)}) copy-start(f32[72]{0:T(128)} %constant.120.clone.1) | copy-start | bytes 868
  230.1 6.9 %collective-permute-start.1 = (f32[72,1024]{1,0:T(8,128)S(1)}, f32[72,1024]{1,0:T(8,128)S(1)}, u32[]{:S(2)}, u32[]{:S(2)}) collective-permute-start(f32[72,1024]{1,0:T(8,128)S(1)} %bitcast.86), channel_id=1, source_target_pairs={{0,1},{1,0},{2,3},{3,2},{4,5},{5,4},{6,7},{7,6},{8,9},{9,8},{10,11... | collective-permute-start | bytes 884744 | tf_op jit(solution)/shard_map/ppermute | solution.py:267
  275.6 26.7 %all-to-all-start.3 = ((bf16[16,304,128]{2,1,0:T(8,128)(2,1)}), bf16[16,304,128]{2,1,0:T(8,128)(2,1)S(1)}, u32[]{:S(2)}, u32[]{:S(2)}) async-start(bf16[16,304,128]{2,1,0:T(8,128)(2,1)} %copy.63), calls=%async_computation.3 | async-start | bytes 2490368 | tf_op jit(solution)/shard_map/all_to_all | solution.py:299
Sparse Core Ops, SparseCore 0:
  10.2 46.0 all-gather.2
  113.2 82.4 all-gather.4

commit v2 on v1

--- a/solution.py
+++ b/solution.py
@@ -148,6 +148,9 @@
             pltpu.VMEM((TILE, seq), jnp.bfloat16),
         ],
         compiler_params=pltpu.CompilerParams(vmem_limit_bytes=40 * 2**20),
+        cost_estimate=pl.CostEstimate(
+            flops=len(tdims) * 10_000_000_000, bytes_accessed=4 * 2**20, transcendentals=0
+        ),
     )(count, half, *town, *sown, *tall, *sall)
 
 
@@ -156,14 +159,11 @@
     return lax.dynamic_index_in_dim(cut, half, 2, keepdims=False).reshape(rows.shape[0], -1)
 
 
-def by_head(query, kv, heads):
-    feats = query.shape[0]
-    parts = [
-        query.reshape(feats, heads, -1),
-        kv[:, 0].reshape(feats, heads, -1),
-        kv[:, 1].reshape(feats, heads, -1),
-    ]
-    return jnp.concatenate(parts, axis=2)
+def columns_of_heads(parts, heads, pad):
+    feats = parts[0].shape[0]
+    joined = jnp.concatenate([a.reshape(feats, heads, -1) for a in parts], axis=2)
+    joined = jnp.pad(joined, ((0, 0), (0, 0), (0, pad - joined.shape[2])))
+    return joined.reshape(feats, -1)
 
 
 def with_mask_row(rows, last):
@@ -194,118 +194,119 @@
     token_ids, teacher_hidden, teacher_query, teacher_kv, student_hidden, student_query, student_kv
 ):
     seq_len = token_ids.shape[0]
-    local_heads = HEADS // lax.axis_size(HEAD)
+    heads = lax.axis_size(HEAD)
+    local_heads = HEADS // heads
     rows = lax.axis_size(ROW)
-    me = lax.axis_index(ROW)
-    half = me % 2
+    half = lax.axis_index(ROW) % 2
+    swap = [(i, i ^ 1) for i in range(lax.axis_size(ROW[1]))]
     valid_mask = token_ids != pad_token
     count = jnp.sum(valid_mask.astype(jnp.int32))
-
-    both = jnp.concatenate([teacher_hidden, student_hidden], axis=1)
-    feats = lax.all_gather(both, HEAD, axis=0, tiled=True)
-    teacher_feats = feats[:, : teacher_hidden.shape[1]]
-    student_feats = feats[:, teacher_hidden.shape[1] :]
-
-    tdims = tuple(
-        c // local_heads for c in (teacher_query.shape[1], teacher_kv.shape[2], teacher_kv.shape[2])
-    )
-    sdims = tuple(
-        c // local_heads for c in (student_query.shape[1], student_kv.shape[2], student_kv.shape[2])
-    )
-    twidth, swidth = sum(tdims), sum(sdims)
-    teacher_weight = by_head(teacher_query, teacher_kv, local_heads)
-    student_weight = by_head(student_query, student_kv, local_heads)
-    student_padded = jnp.pad(student_weight, ((0, 0), (0, 0), (0, -swidth % 16)))
-    swidth_pad = student_padded.shape[2]
-    project = lambda w, x: lax.dot_general(
-        w.reshape(w.shape[0], -1),
-        x,
-        (((0,), (1,)), ((), ())),
-        preferred_element_type=jnp.float32,
-    )
-    student_part = project(student_padded, student_feats)
-    teacher_part = project(teacher_weight, teacher_feats)
+    bias = jnp.where(valid_mask, 0.0, neg_fill)
+    ones = jnp.ones((seq_len // 2,), jnp.float32)
+
+    tq, tk = teacher_query.shape[1] // local_heads, teacher_kv.shape[2] // local_heads
+    sq, sk = student_query.shape[1] // local_heads, student_kv.shape[2] // local_heads
+    q_pad = sq + -sq % 16
+    s_pad = q_pad + 2 * sk
+    student_parts = [student_query, student_kv[:, 0], student_kv[:, 1]]
+    student_weight = columns_of_heads(student_parts, local_heads, s_pad)
+    teacher_kv_weight = columns_of_heads([teacher_kv[:, 0], teacher_kv[:, 1]], local_heads, 2 * tk)
+
+    def project(weight, feats):
+        return lax.dot_general(
+            weight, feats, (((0,), (1,)), ((), ())), preferred_element_type=jnp.float32
+        )
+
+    def swapped(own):
+        other = lax.ppermute(own, ROW[1], swap)
+        low = jnp.where(half == 0, own, other)
+        high = jnp.where(half == 0, other, own)
+        return jnp.concatenate([low, high])
 
     def reduced(part):
         arrived = lax.all_to_all(
             part.reshape(rows, -1, seq_len), ROW, split_axis=0, concat_axis=0, tiled=True
         )
-        return arrived.sum(axis=0).astype(jnp.bfloat16)
-
-    own_half = jnp.concatenate([reduced(teacher_part), reduced(student_part)])
-    swap = [(i, i ^ 1) for i in range(lax.axis_size(ROW[1]))]
-    other = lax.ppermute(own_half, ROW[1], swap)
-    low = jnp.where(half == 0, own_half, other)
-    high = jnp.where(half == 0, other, own_half)
-    tcut = twidth // 2
-    teacher_rows = jnp.concatenate([low[:tcut], high[:tcut]])
-    student_rows = jnp.concatenate([low[tcut:], high[tcut:]])
-
-    def cut(block, dims):
-        out, at = [], 0
-        for d in dims:
-            out.append(block[at : at + d])
-            at += d
-        return out
-
-    bias = jnp.where(valid_mask, 0.0, neg_fill)
-    ones = jnp.ones((seq_len // 2,), jnp.float32)
-    every = lambda parts: [with_mask_row(a, bias) for a in parts]
-    mine = lambda parts: [with_mask_row(own_tokens(a, half), ones) for a in parts]
-    tparts, sparts = cut(teacher_rows, tdims), cut(student_rows, sdims)
-    query_part, key_part, loss = relations(
-        count[None],
-        half[None].astype(jnp.int32),
-        tdims,
-        sdims,
-        mine(tparts),
-        mine(sparts),
-        every(tparts),
-        every(sparts),
-    )
-    loss_sum = jnp.sum(loss[:, 0])
-    from_other = lax.ppermute(own_tokens(key_part, 1 - half), ROW[1], swap)
-    scale = jnp.concatenate([jnp.full((d, 1), d ** (-0.5), jnp.float32) for d in sdims])
-    grad_own = ((query_part + own_tokens(key_part, half) + from_other) * scale).astype(jnp.bfloat16)
-    below = -swidth % 16
-    extra = jnp.zeros((below, grad_own.shape[1]), jnp.bfloat16).at[0, :3].set(pieces(loss_sum))
-    arrived = copy_for_each(jnp.concatenate([grad_own, extra]), ROW)
-    row_loss = jnp.sum(arrived[:, swidth, :3].astype(jnp.float32))
-    grads = (
-        arrived[:, :swidth].reshape(local_heads, 2, swidth, -1, TILE)
-        .transpose(0, 2, 3, 1, 4)
-        .reshape(local_heads * swidth, seq_len)
-    )
-    weight_grad = lax.dot_general(
-        student_feats, grads, (((0,), (1,)), ((), ())), preferred_element_type=jnp.float32
-    ).reshape(student_feats.shape[1], local_heads, swidth)
-    q, k = sdims[0], sdims[1]
-    query_out = weight_grad[:, :, :q].reshape(student_query.shape)
-    kv_out = jnp.stack(
+        return swapped(arrived.sum(axis=0).astype(jnp.bfloat16))
+
+    student_feats = lax.all_gather(student_hidden, HEAD, axis=0, tiled=True)
+    teacher_feats = lax.all_gather(teacher_hidden, HEAD, axis=0, tiled=True)
+    student_rows = reduced(project(student_weight, student_feats))
+    teacher_kv_rows = reduced(project(teacher_kv_weight, teacher_feats))
+    teacher_q_rows = reduced(project(teacher_query, teacher_feats))
+
+    def relate(tparts, sparts):
+        every = lambda parts: [with_mask_row(a, bias) for a in parts]
+        mine = lambda parts: [with_mask_row(own_tokens(a, half), ones) for a in parts]
+        tdims, sdims = tuple(a.shape[0] for a in tparts), tuple(a.shape[0] for a in sparts)
+        query_part, key_part, loss = relations(
+            count[None],
+            half[None].astype(jnp.int32),
+            tdims,
+            sdims,
+            mine(tparts),
+            mine(sparts),
+            every(tparts),
+            every(sparts),
+        )
+        from_other = lax.ppermute(own_tokens(key_part, 1 - half), ROW[1], swap)
+        scale = jnp.concatenate([jnp.full((d, 1), d ** (-0.5), jnp.float32) for d in sdims])
+        grad = (query_part + own_tokens(key_part, half) + from_other) * scale
+        return grad.astype(jnp.bfloat16), jnp.sum(loss[:, 0])
+
+    def shared(grad):
+        arrived = copy_for_each(grad, ROW)
+        cut = arrived.reshape(local_heads, 2, grad.shape[0], -1, TILE // LANES, LANES)
+        return cut.transpose(3, 1, 4, 0, 2, 5).reshape(heads, -1, LANES)
+
+    def weight_grads(blocks):
+        by_column = jnp.moveaxis(blocks, 0, 1).reshape(blocks.shape[1], seq_len)
+        return lax.dot_general(
+            student_feats, by_column, (((0,), (1,)), ((), ())), preferred_element_type=jnp.float32
+        ).reshape(student_feats.shape[1], local_heads, -1)
+
+    def token_grads(blocks, weight):
+        got = lax.all_to_all(blocks, HEAD, split_axis=0, concat_axis=0, tiled=True)
+        flat = got.reshape(-1, got.shape[2])
+        return got, lax.dot_general(
+            flat,
+            weight.reshape(flat.shape[0], -1),
+            (((0,), (0,)), ((), ())),
+            preferred_element_type=jnp.float32,
+        )
+
+    spread = jnp.concatenate(
         [
-            weight_grad[:, :, q : q + k].reshape(-1, local_heads * k),
-            weight_grad[:, :, q + k :].reshape(-1, local_heads * k),
-        ],
-        axis=1,
-    )
-
-    heads = lax.axis_size(HEAD)
-    all_weight = lax.all_gather(
-        student_weight.reshape(student_weight.shape[0], -1).T, HEAD, axis=0, tiled=True
-    )
-    blocks = jnp.moveaxis(grads.reshape(grads.shape[0], heads, -1), 1, 0)
-    extra = jnp.zeros((16, blocks.shape[2]), jnp.bfloat16).at[0, :3].set(pieces(row_loss))
-    sent = jnp.concatenate([blocks, jnp.broadcast_to(extra[None], (heads, *extra.shape))], axis=1)
-    got = lax.all_to_all(sent, HEAD, split_axis=0, concat_axis=0, tiled=True)
-    kl_sum = jnp.sum(got[:, grads.shape[0], :3].astype(jnp.float32))
-    input_grad = lax.dot_general(
-        got[:, : grads.shape[0]].reshape(heads * grads.shape[0], -1),
-        all_weight,
-        (((0,), (0,)), ((), ())),
-        preferred_element_type=jnp.float32,
-    )
+            columns_of_heads(student_parts[:1], local_heads, q_pad).T,
+            columns_of_heads(student_parts[1:], local_heads, 2 * sk).T,
+        ]
+    )
+    all_weight = lax.all_gather(spread, HEAD, axis=0, tiled=False)
+
+    kv_grad, kv_loss = relate(
+        [teacher_kv_rows[:tk], teacher_kv_rows[tk:]],
+        [student_rows[sq : sq + sk], student_rows[sq + sk : sq + 2 * sk]],
+    )
+    kv_blocks = shared(kv_grad)
+    kv_out = (
+        weight_grads(kv_blocks)
+        .reshape(-1, local_heads, 2, sk)
+        .transpose(0, 2, 1, 3)
+        .reshape(student_kv.shape)
+    )
+    _, kv_input = token_grads(kv_blocks, all_weight[:, local_heads * q_pad :])
+
+    q_grad, q_loss = relate([teacher_q_rows], [student_rows[:sq]])
+    loss = q_loss + kv_loss
+    loss = pieces(loss + lax.ppermute(loss, ROW[1], swap))
+    last = jnp.zeros((q_pad - sq, q_grad.shape[1] // LANES, LANES), jnp.bfloat16)
+    last = last.at[0, :, :3].set(jnp.broadcast_to(loss, (last.shape[1], 3)))
+    q_blocks = shared(jnp.concatenate([q_grad, last.reshape(q_pad - sq, -1)]))
+    query_out = weight_grads(q_blocks)[:, :, :sq].reshape(student_query.shape)
+    got, q_input = token_grads(q_blocks, all_weight[:, : local_heads * q_pad])
+    kl_sum = jnp.sum(got.reshape(heads, local_heads, q_pad, LANES)[:, :, sq, :3].astype(jnp.float32))
     mean_kl = kl_sum / (3.0 * HEADS * count.astype(jnp.float32))
-    return (mean_kl, query_out, kv_out, input_grad)
+    return (mean_kl, query_out, kv_out, kv_input + q_input)
 
 
 def solution(mesh):

time: 317 us -> 335 us (1.057)
  waiting for transfers between devices: 139 us -> 179 us
  blocking collectives: 24.3 us -> 0 us
  starting transfers between devices: 37 us -> 49.9 us
  local copies, waits for them, and re-layouts: 27.6 us -> 18.3 us
  matrix products: 19.5 us -> 25.7 us
  between operations: 27.8 us -> 22.8 us
  other arithmetic: 14.7 us -> 9.94 us
    ppermute x2 -> x6, waiting for transfers between devices: 8.31 us -> 61 us  [the longest x3 61 us: swapped(): other = lax.ppermute(own, ROW[1], swap)]
    all_to_all x2 -> x3, waiting for transfers between devices: 74.1 us -> 49.5 us  [reduced(): lax.all_to_all(part.reshape(rows, -1, seq_len), ROW, split_axis=0, concat...]
    all_to_all x1 -> x0, blocking collectives: 24.3 us -> none  [copy_for_each(): lax.all_to_all(jnp.broadcast_to(value[None], (size, *value.shape)), axis,...]
    all_to_all x1 -> x4, starting transfers between devices: 8.82 us -> 25.4 us  [the longest x2 15.3 us: token_grads(): got = lax.all_to_all(blocks, HEAD, split_axis=0, concat_axis=0, tiled=True)]
    all_to_all x1 -> x4, waiting for transfers between devices: 11.1 us -> 19.4 us  [the longest x2 11.1 us: copy_for_each(): lax.all_to_all(jnp.broadcast_to(value[None], (size, *value.shape)), axis,...]
    dot_general x4 -> x7, matrix products: 19.5 us -> 25.7 us  [the longest x3 15.3 us: project(): lax.dot_general(weight, feats, (((0,), (1,)), ((), ())), preferred_elemen...]
    concatenate x8 -> x7, other arithmetic: 6.53 us -> 0.89 us  [the longest x1 0.76 us: per_device(): jnp.concatenate([columns_of_heads(student_parts[:1], local_heads, q_pad)....]
    concatenate x2 -> x0, local copies, waits for them, and re-layouts: 5.59 us -> none  [the longest x1 4.22 us: by_head(): return jnp.concatenate(parts, axis=2)]
  transfers between devices with their start and end apart: 7 -> 16, of which waited for: 5 -> 10; matrix products, arithmetic and copies ran while one was open for 16% -> 14% of each run, Pallas kernels for 9% -> 8%
where the time goes in v2:
time: 335 us; the launch traced here: 334 us
  waiting for transfers between devices  179 us (53%)
  starting transfers between devices  49.9 us (15%)
  Pallas kernels  28.3 us (8%)
  matrix products  25.7 us (8%)
  between operations  22.8 us (7%)
  local copies, waits for them, and re-layouts  18.3 us (5%)
  other arithmetic  9.94 us (3%)
    ppermute x3, waiting for transfers between devices, swapped(): other = lax.ppermute(own, ROW[1], swap)  61 us
    all_to_all x3, waiting for transfers between devices, reduced(): lax.all_to_all(part.reshape(rows, -1, seq_len), ROW, split_axis=0, concat...  49.5 us
    all_gather x1, waiting for transfers between devices, per_device(): student_feats = lax.all_gather(student_hidden, HEAD, axis=0, tiled=True)  38.8 us
    pallas_call x2, Pallas kernels, relations(): pl.pallas_call(functools.partial(relation_kernel, tdims, sdims), grid=(mi...  28.3 us
    all_to_all x3, starting transfers between devices, reduced(): lax.all_to_all(part.reshape(rows, -1, seq_len), ROW, split_axis=0, concat...  17.6 us
    all_to_all x2, starting transfers between devices, token_grads(): got = lax.all_to_all(blocks, HEAD, split_axis=0, concat_axis=0, tiled=True)  15.3 us
    dot_general x3, matrix products, project(): lax.dot_general(weight, feats, (((0,), (1,)), ((), ())), preferred_elemen...  15.3 us
    all_to_all x2, waiting for transfers between devices, copy_for_each(): lax.all_to_all(jnp.broadcast_to(value[None], (size, *value.shape)), axis,...  11.1 us
  transfers between devices with their start and end apart: 16, of which 10 were waited for; matrix products, arithmetic and copies ran while one was open for 14% of the time, Pallas kernels for 8%

profile of v2, /device:TPU:1, one launch (start us, length us, event | category | flops | bytes accessed | tf_op | source)
XLA Modules:
  0.0 334.0 jit_solution(4289926741324200674)
XLA Ops:
  10.6 38.8 %all-gather.7.cloned.1.call-done = bf16[2048,448]{0,1:T(8,128)(2,1)} async-done(((bf16[128,448]{0,1:T(8,128)(2,1)}), bf16[2048,448]{0,1:T(8,128)(2,1)}) %all-gather.7.cloned.1.call-update) | async-done | bytes 1835024 | tf_op jit(solution)/shard_map/all_gather | solution.py:232
  49.3 3.9 %fusion.4 = f32[8,40,2048]{2,1,0:T(8,128)} fusion(bf16[8,40,448]{2,1,0:T(8,128)(2,1)S(1)} %bitcast.106, bf16[2048,448]{0,1:T(8,128)(2,1)} %all-gather.7.cloned.1.call-done), kind=kOutput, calls=%fused_computation.4 | convolution fusion | flops 587202560 | bytes 4743168 | tf_op jit(solution)/shard_map/dot_general | solution.py:216
  53.2 6.4 %all-to-all-start.1 = ((f32[8,40,2048]{2,1,0:T(8,128)}), f32[8,40,2048]{2,1,0:T(8,128)}, u32[]{:S(2)}, u32[]{:S(2)}) async-start(f32[8,40,2048]{2,1,0:T(8,128)} %fusion.4), calls=%async_computation.1 | async-start | bytes 5242880 | tf_op jit(solution)/shard_map/all_to_all | solution.py:227
  60.6 38.2 %all-to-all-done.1 = f32[8,40,2048]{2,1,0:T(8,128)} async-done(((f32[8,40,2048]{2,1,0:T(8,128)}), f32[8,40,2048]{2,1,0:T(8,128)}, u32[]{:S(2)}, u32[]{:S(2)}) %all-to-all-start.1) | async-done | bytes 2621472 | tf_op jit(solution)/shard_map/all_to_all | solution.py:227
  102.7 2.8 collective-permute-done.1
  105.5 8.9 %all-gather.5.cloned.1.call-done = bf16[2048,1024]{1,0:T(8,128)(2,1)} async-done(((bf16[128,1024]{1,0:T(8,128)(2,1)}), bf16[2048,1024]{1,0:T(8,128)(2,1)}) %all-gather.5.cloned.1.call-update) | async-done | bytes 4194320 | tf_op jit(solution)/shard_map/all_gather | solution.py:233
  114.4 4.7 %fusion.2 = f32[8,16,2048]{2,1,0:T(8,128)} fusion(bf16[8,16,1024]{2,1,0:T(8,128)(2,1)S(1)} %bitcast.111, bf16[2048,1024]{1,0:T(8,128)(2,1)} %all-gather.5.cloned.1.call-done), kind=kOutput, calls=%fused_computation.2 | convolution fusion | flops 536870912 | bytes 5505024 | tf_op jit(solution)/shard_map/dot_general | solution.py:216
  119.0 6.6 %all-to-all-start.2 = ((f32[8,16,2048]{2,1,0:T(8,128)}), f32[8,16,2048]{2,1,0:T(8,128)S(1)}, u32[]{:S(2)}, u32[]{:S(2)}) async-start(f32[8,16,2048]{2,1,0:T(8,128)} %fusion.2), calls=%async_computation.2 | async-start | bytes 2097152 | tf_op jit(solution)/shard_map/all_to_all | solution.py:227
  125.6 6.7 %fusion.24 = f32[512,2048]{1,0:T(8,128)} fusion(bf16[1024,512]{1,0:T(8,128)(2,1)S(1)} %copy-done, bf16[2048,1024]{1,0:T(8,128)(2,1)} %all-gather.5.cloned.1.call-done), kind=kOutput, calls=%fused_computation.78 | convolution fusion | flops 2147483648 | bytes 9437184 | tf_op jit(solution)/shard_map/dot_general | solution.py:216
  132.3 11.3 %all-to-all-done.2 = f32[8,16,2048]{2,1,0:T(8,128)S(1)} async-done(((f32[8,16,2048]{2,1,0:T(8,128)}), f32[8,16,2048]{2,1,0:T(8,128)S(1)}, u32[]{:S(2)}, u32[]{:S(2)}) %all-to-all-start.2) | async-done | bytes 1048608 | tf_op jit(solution)/shard_map/all_to_all | solution.py:227
  143.6 4.6 %all-to-all-start = ((f32[8,64,2048]{2,1,0:T(8,128)}), f32[8,64,2048]{2,1,0:T(8,128)}, u32[]{:S(2)}, u32[]{:S(2)}) async-start(f32[8,64,2048]{2,1,0:T(8,128)} %bitcast.100), calls=%async_computation | async-start | bytes 8388608 | tf_op jit(solution)/shard_map/all_to_all | solution.py:227
  150.8 58.0 %collective-permute-done.3 = bf16[16,2048]{1,0:T(8,128)(2,1)S(1)} collective-permute-done((bf16[16,2048]{1,0:T(8,128)(2,1)S(1)}, bf16[16,2048]{1,0:T(8,128)(2,1)S(1)}, u32[]{:S(2)}, u32[]{:S(2)}) %collective-permute-start.3) | collective-permute-done | bytes 65568 | tf_op jit(solution)/shard_map/ppermute | solution.py:221
  209.4 18.2 %shard_map.103 = (f32[16,1024]{1,0:T(8,128)S(1)}, f32[16,2048]{1,0:T(8,128)S(1)}, f32[32,128]{1,0:T(8,128)S(1)}) custom-call(s32[1]{0:T(128)} %bitcast.n_ref, s32[1]{0:T(128)} %bitcast.1.p_ref, bf16[32,1024]{1,0:T(8,128)(2,1)S(1)} %get-tuple-element.55.refs_0_, bf16[32,1024]{1,0:T(8,128)(2,1)S(1)} %get-tuple-element.54.refs_1_, ...), custom_call_target="tpu_custom_call" | custom-call | flops 20000000000 | bytes 4194304 | tf_op jit(solution)/shard_map/pallas_call | solution.py:127
  228.3 2.5 reduce_sum.64
  234.0 3.7 %all-to-all-start.5 = ((bf16[8,16,1024]{2,1,0:T(8,128)(2,1)}), bf16[8,16,1024]{2,1,0:T(8,128)(2,1)S(1)}, u32[]{:S(2)}, u32[]{:S(2)}) async-start(bf16[8,16,1024]{2,1,0:T(8,128)(2,1)} %broadcast_in_dim.21), calls=%async_computation.5 | async-start | bytes 524288 | tf_op jit(solution)/shard_map/all_to_all | solution.py:188
  239.7 10.1 %shard_map.102 = (f32[56,1024]{1,0:T(8,128)S(1)}, f32[56,2048]{1,0:T(8,128)S(1)}, f32[32,128]{1,0:T(8,128)S(1)}) custom-call(s32[1]{0:T(128)} %bitcast.n_ref, s32[1]{0:T(128)} %bitcast.1.p_ref, bf16[144,1024]{1,0:T(8,128)(2,1)S(1)} %pad_maximum_fusion.3.refs_0_, bf16[64,1024]{1,0:T(8,128)(2,1)S(1)} %pad_maximum_fusion.11.refs_1_, ...), custom_call_target="tpu_custom_call" | custom-call | flops 10000000000 | bytes 4194304 | tf_op jit(solution)/shard_map/pallas_call | solution.py:127
  262.7 6.4 %all-to-all-start.3 = ((bf16[8,64,1024]{2,1,0:T(8,128)(2,1)}), bf16[8,64,1024]{2,1,0:T(8,128)(2,1)S(1)}, u32[]{:S(2)}, u32[]{:S(2)}) async-start(bf16[8,64,1024]{2,1,0:T(8,128)(2,1)} %broadcast_in_dim.20), calls=%async_computation.3 | async-start | bytes 2097152 | tf_op jit(solution)/shard_map/all_to_all | solution.py:188
  270.0 11.1 %all-to-all-done.3 = bf16[8,64,1024]{2,1,0:T(8,128)(2,1)S(1)} async-done(((bf16[8,64,1024]{2,1,0:T(8,128)(2,1)}), bf16[8,64,1024]{2,1,0:T(8,128)(2,1)S(1)}, u32[]{:S(2)}, u32[]{:S(2)}) %all-to-all-start.3) | async-done | bytes 1048608 | tf_op jit(solution)/shard_map/all_to_all | solution.py:188
  281.1 10.5 %all-to-all-start.6 = ((bf16[16,64,128]{2,1,0:T(8,128)(2,1)}), bf16[16,64,128]{2,1,0:T(8,128)(2,1)S(1)}, u32[]{:S(2)}, u32[]{:S(2)}) async-start(bf16[16,64,128]{2,1,0:T(8,128)(2,1)} %bitcast.35), calls=%async_computation.6 | async-start | bytes 524288 | tf_op jit(solution)/shard_map/all_to_all | solution.py:269
  293.1 2.6 copy.23
  295.8 3.1 all-to-all-done.6
  298.8 4.8 %all-to-all-start.4 = ((bf16[16,256,128]{2,1,0:T(8,128)(2,1)}), bf16[16,256,128]{2,1,0:T(8,128)(2,1)}, u32[]{:S(2)}, u32[]{:S(2)}) async-start(bf16[16,256,128]{2,1,0:T(8,128)(2,1)} %bitcast.27), calls=%async_computation.4 | async-start | bytes 2097152 | tf_op jit(solution)/shard_map/all_to_all | solution.py:269
  314.4 5.2 %all-to-all-done.4 = bf16[16,256,128]{2,1,0:T(8,128)(2,1)} async-done(((bf16[16,256,128]{2,1,0:T(8,128)(2,1)}), bf16[16,256,128]{2,1,0:T(8,128)(2,1)}, u32[]{:S(2)}, u32[]{:S(2)}) %all-to-all-start.4) | async-done | bytes 1048608 | tf_op jit(solution)/shard_map/all_to_all | solution.py:269
  321.8 4.5 %fusion.9 = f32[128,448]{0,1:T(8,128)} fusion(f32[128,448]{0,1:T(8,128)S(1)} %copy-done.4, bf16[16,256,128]{2,1,0:T(8,128)(2,1)} %all-to-all-done.4, bf16[16,320,448]{2,1,0:T(8,128)(2,1)} %bitcast.136), kind=kOutput, calls=%fused_computation.9 | convolution fusion | flops 469819392 | bytes 5701632 | tf_op jit(solution)/shard_map/dot_general | solution.py:271
  (104 shorter events, 37.6 us)
Async XLA Ops:
  7.2 118.5 %copy-start = (bf16[1024,512]{1,0:T(8,128)(2,1)S(1)}, bf16[1024,512]{1,0:T(8,128)(2,1)}, u32[]{:S(2)}) copy-start(bf16[1024,512]{1,0:T(8,128)(2,1)} %param.11) | copy-start | bytes 3145732
  7.2 42.2 %all-gather.7.cloned.1.call-start = ((), (), s32[]{:S(2)}) async-start(), calls=%async_computation.8 | async-start | bytes 1949696 | tf_op jit(solution)/shard_map/all_gather | solution.py:232
  7.9 106.5 %all-gather.5.cloned.1.call-start = ((), (), s32[]{:S(2)}) async-start(), calls=%async_computation.7 | async-start | bytes 4456448 | tf_op jit(solution)/shard_map/all_gather | solution.py:233
  53.2 7.3 %copy-start.3 = (s32[2048]{0:T(1024)S(1)}, s32[2048]{0:T(1024)}, u32[]{:S(2)}) copy-start(s32[2048]{0:T(1024)} %param.9) | copy-start | bytes 24580
  53.2 7.3 %copy-start.2 = (bf16[1024,2,64]{0,2,1:T(8,128)(2,1)S(1)}, bf16[1024,2,64]{0,2,1:T(8,128)(2,1)}, u32[]{:S(2)}) copy-start(bf16[1024,2,64]{0,2,1:T(8,128)(2,1)} %param.12) | copy-start | bytes 786436
  53.2 45.6 %all-to-all-start.1 = ((f32[8,40,2048]{2,1,0:T(8,128)}), f32[8,40,2048]{2,1,0:T(8,128)}, u32[]{:S(2)}, u32[]{:S(2)}) async-start(f32[8,40,2048]{2,1,0:T(8,128)} %fusion.4), calls=%async_computation.1 | async-start | bytes 5242880 | tf_op jit(solution)/shard_map/all_to_all | solution.py:227
  59.6 246.9 %all-gather.9.cloned.1.call-start = ((), (), s32[]{:S(2)}) async-start(), calls=%async_computation.9 | async-start | bytes 5570560 | tf_op jit(solution)/shard_map/all_gather | solution.py:284
  100.8 4.6 %collective-permute-start.1 = (bf16[40,2048]{1,0:T(8,128)(2,1)S(1)}, bf16[40,2048]{1,0:T(8,128)(2,1)S(1)}, u32[]{:S(2)}, u32[]{:S(2)}) collective-permute-start(bf16[40,2048]{1,0:T(8,128)(2,1)S(1)} %reduce_sum.65), channel_id=1, source_target_pairs={{0,1},{1,0},{2,3},{3,2},{4,5},{5,4},{6,7},{7,6},{8,9},{9,8},{10,11... | collective-permute-start | bytes 491528 | tf_op jit(solution)/shard_map/ppermute | solution.py:221
  119.0 24.5 %all-to-all-start.2 = ((f32[8,16,2048]{2,1,0:T(8,128)}), f32[8,16,2048]{2,1,0:T(8,128)S(1)}, u32[]{:S(2)}, u32[]{:S(2)}) async-start(f32[8,16,2048]{2,1,0:T(8,128)} %fusion.2), calls=%async_computation.2 | async-start | bytes 2097152 | tf_op jit(solution)/shard_map/all_to_all | solution.py:227
  143.6 84.7 %all-to-all-start = ((f32[8,64,2048]{2,1,0:T(8,128)}), f32[8,64,2048]{2,1,0:T(8,128)}, u32[]{:S(2)}, u32[]{:S(2)}) async-start(f32[8,64,2048]{2,1,0:T(8,128)} %bitcast.100), calls=%async_computation | async-start | bytes 8388608 | tf_op jit(solution)/shard_map/all_to_all | solution.py:227
  149.3 59.5 %collective-permute-start.3 = (bf16[16,2048]{1,0:T(8,128)(2,1)S(1)}, bf16[16,2048]{1,0:T(8,128)(2,1)S(1)}, u32[]{:S(2)}, u32[]{:S(2)}) collective-permute-start(bf16[16,2048]{1,0:T(8,128)(2,1)S(1)} %reduce_sum.67), channel_id=1, source_target_pairs={{0,1},{1,0},{2,3},{3,2},{4,5},{5,4},{6,7},{7,6},{8,9},{9,8},{10,11... | collective-permute-start | bytes 196616 | tf_op jit(solution)/shard_map/ppermute | solution.py:221
  228.2 4.9 %collective-permute-start.5 = (f32[16,1024]{1,0:T(8,128)S(1)}, f32[16,1024]{1,0:T(8,128)S(1)}, u32[]{:S(2)}, u32[]{:S(2)}) collective-permute-start(f32[16,1024]{1,0:T(8,128)S(1)} %bitcast.132), channel_id=1, source_target_pairs={{0,1},{1,0},{2,3},{3,2},{4,5},{5,4},{6,7},{7,6},{8,9},{9,8},{10,11... | collective-permute-start | bytes 196616 | tf_op jit(solution)/shard_map/ppermute | solution.py:252
  230.8 7.1 %collective-permute-start = (bf16[64,2048]{1,0:T(8,128)(2,1)S(1)}, bf16[64,2048]{1,0:T(8,128)(2,1)S(1)}, u32[]{:S(2)}, u32[]{:S(2)}) collective-permute-start(bf16[64,2048]{1,0:T(8,128)(2,1)S(1)} %reduce_sum.64), channel_id=1, source_target_pairs={{0,1},{1,0},{2,3},{3,2},{4,5},{5,4},{6,7},{7,6},{8,9},{9,8},{10,11... | collective-permute-start | bytes 786440 | tf_op jit(solution)/shard_map/ppermute | solution.py:221
  234.0 27.6 %all-to-all-start.5 = ((bf16[8,16,1024]{2,1,0:T(8,128)(2,1)}), bf16[8,16,1024]{2,1,0:T(8,128)(2,1)S(1)}, u32[]{:S(2)}, u32[]{:S(2)}) async-start(bf16[8,16,1024]{2,1,0:T(8,128)(2,1)} %broadcast_in_dim.21), calls=%async_computation.5 | async-start | bytes 524288 | tf_op jit(solution)/shard_map/all_to_all | solution.py:188
  251.7 4.2 %collective-permute-start.4 = (f32[]{:T(128)}, f32[]{:T(128)}, u32[]{:S(2)}, u32[]{:S(2)}) collective-permute-start(f32[]{:T(128)} %add.63), channel_id=1, source_target_pairs={{0,1},{1,0},{2,3},{3,2},{4,5},{5,4},{6,7},{7,6},{8,9},{9,8},{10,11... | collective-permute-start | bytes 20 | tf_op jit(solution)/shard_map/ppermute | solution.py:301
  255.5 5.9 %collective-permute-start.2 = (f32[56,1024]{1,0:T(8,128)S(1)}, f32[56,1024]{1,0:T(8,128)S(1)}, u32[]{:S(2)}, u32[]{:S(2)}) collective-permute-start(f32[56,1024]{1,0:T(8,128)S(1)} %bitcast.124), channel_id=1, source_target_pairs={{0,1},{1,0},{2,3},{3,2},{4,5},{5,4},{6,7},{7,6},{8,9},{9,8},{10,11... | collective-permute-start | bytes 688136 | tf_op jit(solution)/shard_map/ppermute | solution.py:252
  262.7 18.5 %all-to-all-start.3 = ((bf16[8,64,1024]{2,1,0:T(8,128)(2,1)}), bf16[8,64,1024]{2,1,0:T(8,128)(2,1)S(1)}, u32[]{:S(2)}, u32[]{:S(2)}) async-start(bf16[8,64,1024]{2,1,0:T(8,128)(2,1)} %broadcast_in_dim.20), calls=%async_computation.3 | async-start | bytes 2097152 | tf_op jit(solution)/shard_map/all_to_all | solution.py:188
  281.1 17.7 %all-to-all-start.6 = ((bf16[16,64,128]{2,1,0:T(8,128)(2,1)}), bf16[16,64,128]{2,1,0:T(8,128)(2,1)S(1)}, u32[]{:S(2)}, u32[]{:S(2)}) async-start(bf16[16,64,128]{2,1,0:T(8,128)(2,1)} %bitcast.35), calls=%async_computation.6 | async-start | bytes 524288 | tf_op jit(solution)/shard_map/all_to_all | solution.py:269
  293.1 11.1 %copy-start.1 = (bf16[2048,448]{0,1:T(8,128)(2,1)S(1)}, bf16[2048,448]{0,1:T(8,128)(2,1)}, u32[]{:S(2)}) copy-start(bf16[2048,448]{0,1:T(8,128)(2,1)} %all-gather.7.cloned.1.call-done) | copy-start | bytes 5505028
  298.8 20.8 %all-to-all-start.4 = ((bf16[16,256,128]{2,1,0:T(8,128)(2,1)}), bf16[16,256,128]{2,1,0:T(8,128)(2,1)}, u32[]{:S(2)}, u32[]{:S(2)}) async-start(bf16[16,256,128]{2,1,0:T(8,128)(2,1)} %bitcast.27), calls=%async_computation.4 | async-start | bytes 2097152 | tf_op jit(solution)/shard_map/all_to_all | solution.py:269
  313.2 8.6 %copy-start.4 = (f32[128,448]{0,1:T(8,128)S(1)}, f32[128,448]{0,1:T(8,128)}, u32[]{:S(2)}) copy-start(f32[128,448]{0,1:T(8,128)} %convolution_bitcast_fusion.1) | copy-start | bytes 688132
Sparse Core Ops, SparseCore 0:
  9.6 39.6 all-gather.6
  51.0 63.2 all-gather.4
  116.7 92.5 all-gather.8

commit v3 on v2

--- a/solution.py
+++ b/solution.py
@@ -224,16 +224,30 @@
         return jnp.concatenate([low, high])
 
     def reduced(part):
-        arrived = lax.all_to_all(
-            part.reshape(rows, -1, seq_len), ROW, split_axis=0, concat_axis=0, tiled=True
-        )
-        return swapped(arrived.sum(axis=0).astype(jnp.bfloat16))
-
-    student_feats = lax.all_gather(student_hidden, HEAD, axis=0, tiled=True)
-    teacher_feats = lax.all_gather(teacher_hidden, HEAD, axis=0, tiled=True)
-    student_rows = reduced(project(student_weight, student_feats))
-    teacher_kv_rows = reduced(project(teacher_kv_weight, teacher_feats))
-    teacher_q_rows = reduced(project(teacher_query, teacher_feats))
+        arrived = lax.all_to_all(part, ROW, split_axis=0, concat_axis=0, tiled=True)
+        return arrived.sum(axis=0).astype(jnp.bfloat16)
+
+    for_rows = lambda part: part.reshape(rows, -1, seq_len)
+    both = jnp.concatenate([teacher_hidden, student_hidden], axis=1)
+    feats = lax.all_gather(both, HEAD, axis=0, tiled=True)
+    teacher_feats = feats[:, : teacher_hidden.shape[1]]
+    student_feats = feats[:, teacher_hidden.shape[1] :]
+    first = jnp.concatenate(
+        [
+            for_rows(project(student_weight, student_feats)),
+            for_rows(project(teacher_kv_weight, teacher_feats)),
+        ],
+        axis=1,
+    )
+    first_rows = swapped(reduced(first))
+    cut = first_rows.reshape(2, -1, seq_len)
+    student_rows = cut[:, : local_heads * s_pad // rows].reshape(-1, seq_len)
+    teacher_kv_rows = cut[:, local_heads * s_pad // rows :].reshape(-1, seq_len)
+    second = for_rows(project(teacher_query, teacher_feats))
+    second, student_rows, teacher_kv_rows = lax.optimization_barrier(
+        (second, student_rows, teacher_kv_rows)
+    )
+    teacher_q_rows = swapped(reduced(second))
 
     def relate(tparts, sparts):
         every = lambda parts: [with_mask_row(a, bias) for a in parts]

time: 335 us -> 316 us (0.943)
  waiting for transfers between devices: 179 us -> 139 us
  starting transfers between devices: 49.9 us -> 59.9 us
  Pallas kernels: 28.3 us -> 37.2 us
    ppermute x3 -> x2, waiting for transfers between devices: 61 us -> 0.01 us  [swapped(): other = lax.ppermute(own, ROW[1], swap)]
    all_to_all x3 -> x2, waiting for transfers between devices: 49.5 us -> 67.3 us  [reduced(): arrived = lax.all_to_all(part, ROW, split_axis=0, concat_axis=0, tiled=True)]
    pallas_call x2, Pallas kernels: 28.3 us -> 37.2 us  [relations(): pl.pallas_call(functools.partial(relation_kernel, tdims, sdims), grid=(mi...]
    ppermute x3 -> x2, starting transfers between devices: 4.35 us -> 12.9 us  [swapped(): other = lax.ppermute(own, ROW[1], swap)]
    all_gather x2 -> x1, waiting for transfers between devices: 47.7 us -> 53.5 us  [per_device(): feats = lax.all_gather(both, HEAD, axis=0, tiled=True)]
    all_to_all x2, starting transfers between devices: 10.1 us -> 14.6 us  [copy_for_each(): lax.all_to_all(jnp.broadcast_to(value[None], (size, *value.shape)), axis,...]
    all_to_all x3 -> x2, starting transfers between devices: 17.6 us -> 13.8 us  [reduced(): arrived = lax.all_to_all(part, ROW, split_axis=0, concat_axis=0, tiled=True)]
    concatenate x0 -> x2, other arithmetic: none -> 3.72 us  [the longest x1 2.05 us: per_device(): jnp.concatenate([for_rows(project(student_weight, student_feats)), for_ro...]
  transfers between devices with their start and end apart: 16 -> 13, of which waited for: 10 -> 6; matrix products, arithmetic and copies ran while one was open for 14% -> 13% of each run, Pallas kernels for 8% -> 12%
where the time goes in v3:
time: 316 us
  waiting for transfers between devices  139 us (44%)
  starting transfers between devices  59.9 us (19%)
  Pallas kernels  37.2 us (12%)
  matrix products  23.1 us (7%)
  between operations  23.1 us (7%)
  local copies, waits for them, and re-layouts  20.3 us (6%)
  other arithmetic  13.1 us (4%)
    all_to_all x2, waiting for transfers between devices, reduced(): arrived = lax.all_to_all(part, ROW, split_axis=0, concat_axis=0, tiled=True)  67.3 us
    all_gather x1, waiting for transfers between devices, per_device(): feats = lax.all_gather(both, HEAD, axis=0, tiled=True)  53.5 us
    pallas_call x2, Pallas kernels, relations(): pl.pallas_call(functools.partial(relation_kernel, tdims, sdims), grid=(mi...  37.2 us
    all_to_all x2, starting transfers between devices, token_grads(): got = lax.all_to_all(blocks, HEAD, split_axis=0, concat_axis=0, tiled=True)  14.6 us
    all_to_all x2, starting transfers between devices, copy_for_each(): lax.all_to_all(jnp.broadcast_to(value[None], (size, *value.shape)), axis,...  14.6 us
    all_to_all x2, starting transfers between devices, reduced(): arrived = lax.all_to_all(part, ROW, split_axis=0, concat_axis=0, tiled=True)  13.8 us
    ppermute x2, starting transfers between devices, swapped(): other = lax.ppermute(own, ROW[1], swap)  12.9 us
    dot_general x3, matrix products, project(): lax.dot_general(weight, feats, (((0,), (1,)), ((), ())), preferred_elemen...  11.9 us
  transfers between devices with their start and end apart: 13, of which 6 were waited for; matrix products, arithmetic and copies ran while one was open for 13% of the time, Pallas kernels for 12%

profile of v3, /device:TPU:1, one launch (start us, length us, event | category | flops | bytes accessed | tf_op | source)
XLA Modules:
  0.0 315.9 jit_solution(16941114972064519792)
XLA Ops:
  13.0 53.5 %all-gather.4.cloned.1.call-done = bf16[2048,1472]{0,1:T(8,128)(2,1)} async-done(((bf16[128,1472]{0,1:T(8,128)(2,1)}), bf16[2048,1472]{0,1:T(8,128)(2,1)}) %all-gather.4.cloned.1.call-update) | async-done | bytes 6029328 | tf_op jit(solution)/shard_map/all_gather | solution.py:232
  66.6 2.9 fusion.2
  69.5 2.4 fusion.11
  73.9 5.8 %all-to-all-start = ((f32[8,56,2048]{2,1,0:T(8,128)}), f32[8,56,2048]{2,1,0:T(8,128)}, u32[]{:S(2)}, u32[]{:S(2)}) async-start(f32[8,56,2048]{2,1,0:T(8,128)} %pad_maximum_fusion), calls=%async_computation | async-start | bytes 7340032 | tf_op jit(solution)/shard_map/all_to_all | solution.py:227
  81.3 44.0 %all-to-all-done = f32[8,56,2048]{2,1,0:T(8,128)} async-done(((f32[8,56,2048]{2,1,0:T(8,128)}), f32[8,56,2048]{2,1,0:T(8,128)}, u32[]{:S(2)}, u32[]{:S(2)}) %all-to-all-start) | async-done | bytes 3670048 | tf_op jit(solution)/shard_map/all_to_all | solution.py:227
  125.2 2.4 reduce_sum.55
  127.6 7.9 %collective-permute-start = (bf16[56,2048]{1,0:T(8,128)(2,1)S(1)}, bf16[56,2048]{1,0:T(8,128)(2,1)S(1)}, u32[]{:S(2)}, u32[]{:S(2)}) collective-permute-start(bf16[56,2048]{1,0:T(8,128)(2,1)S(1)} %reduce_sum.55), channel_id=1, source_target_pairs={{0,1},{1,0},{2,3},{3,2},{4,5},{5,4},{6,7},{7,6},{8,9},{9,8},{10,11... | collective-permute-start | bytes 688136 | tf_op jit(solution)/shard_map/ppermute | solution.py:221
  135.5 6.6 %fusion.5 = f32[2048,512]{0,1:T(8,128)} fusion(bf16[1024,512]{1,0:T(8,128)(2,1)S(1)} %copy-done, bf16[2048,1472]{0,1:T(8,128)(2,1)} %all-gather.4.cloned.1.call-done), kind=kOutput, calls=%fused_computation.5 | convolution fusion | flops 2147483648 | bytes 9437184 | tf_op jit(solution)/shard_map/dot_general | solution.py:216
  142.3 8.0 %all-to-all-start.1 = ((f32[8,64,2048]{2,1,0:T(8,128)}), f32[8,64,2048]{2,1,0:T(8,128)}, u32[]{:S(2)}, u32[]{:S(2)}) async-start(f32[8,64,2048]{2,1,0:T(8,128)} %bitcast.100), calls=%async_computation.1 | async-start | bytes 8388608 | tf_op jit(solution)/shard_map/all_to_all | solution.py:227
  151.9 24.1 %shard_map.103 = (f32[16,1024]{1,0:T(8,128)S(1)}, f32[16,2048]{1,0:T(8,128)S(1)}, f32[32,128]{1,0:T(8,128)S(1)}) custom-call(s32[1]{0:T(128)} %bitcast.n_ref, s32[1]{0:T(128)} %bitcast.1.p_ref, bf16[32,1024]{1,0:T(8,128)(2,1)S(1)} %get-tuple-element.65.refs_0_, bf16[32,1024]{1,0:T(8,128)(2,1)S(1)} %get-tuple-element.64.refs_1_, ...), custom_call_target="tpu_custom_call" | custom-call | flops 20000000000 | bytes 4194304 | tf_op jit(solution)/shard_map/pallas_call | solution.py:127
  178.1 23.3 %all-to-all-done.1 = f32[8,64,2048]{2,1,0:T(8,128)} async-done(((f32[8,64,2048]{2,1,0:T(8,128)}), f32[8,64,2048]{2,1,0:T(8,128)}, u32[]{:S(2)}, u32[]{:S(2)}) %all-to-all-start.1) | async-done | bytes 4194336 | tf_op jit(solution)/shard_map/all_to_all | solution.py:227
  201.4 2.5 reduce_sum.56
  204.0 5.0 %collective-permute-start.1 = (bf16[64,2048]{1,0:T(8,128)(2,1)S(1)}, bf16[64,2048]{1,0:T(8,128)(2,1)S(1)}, u32[]{:S(2)}, u32[]{:S(2)}) collective-permute-start(bf16[64,2048]{1,0:T(8,128)(2,1)S(1)} %reduce_sum.56), channel_id=1, source_target_pairs={{0,1},{1,0},{2,3},{3,2},{4,5},{5,4},{6,7},{7,6},{8,9},{9,8},{10,11... | collective-permute-start | bytes 786440 | tf_op jit(solution)/shard_map/ppermute | solution.py:221
  210.4 8.0 %all-to-all-start.4 = ((bf16[8,16,1024]{2,1,0:T(8,128)(2,1)}), bf16[8,16,1024]{2,1,0:T(8,128)(2,1)S(1)}, u32[]{:S(2)}, u32[]{:S(2)}) async-start(bf16[8,16,1024]{2,1,0:T(8,128)(2,1)} %broadcast_in_dim.21), calls=%async_computation.4 | async-start | bytes 524288 | tf_op jit(solution)/shard_map/all_to_all | solution.py:188
  220.1 13.2 %shard_map.102 = (f32[56,1024]{1,0:T(8,128)S(1)}, f32[56,2048]{1,0:T(8,128)S(1)}, f32[32,128]{1,0:T(8,128)S(1)}) custom-call(s32[1]{0:T(128)} %bitcast.n_ref, s32[1]{0:T(128)} %bitcast.1.p_ref, bf16[144,1024]{1,0:T(8,128)(2,1)S(1)} %pad_maximum_fusion.6.refs_0_, bf16[64,1024]{1,0:T(8,128)(2,1)S(1)} %pad_maximum_fusion.13.refs_1_, ...), custom_call_target="tpu_custom_call" | custom-call | flops 10000000000 | bytes 4194304 | tf_op jit(solution)/shard_map/pallas_call | solution.py:127
  235.2 2.3 collective-permute-start.3
  246.1 6.6 %all-to-all-start.2 = ((bf16[8,64,1024]{2,1,0:T(8,128)(2,1)}), bf16[8,64,1024]{2,1,0:T(8,128)(2,1)S(1)}, u32[]{:S(2)}, u32[]{:S(2)}) async-start(bf16[8,64,1024]{2,1,0:T(8,128)(2,1)} %broadcast_in_dim.20), calls=%async_computation.2 | async-start | bytes 2097152 | tf_op jit(solution)/shard_map/all_to_all | solution.py:188
  253.6 11.0 %all-to-all-done.2 = bf16[8,64,1024]{2,1,0:T(8,128)(2,1)S(1)} async-done(((bf16[8,64,1024]{2,1,0:T(8,128)(2,1)}), bf16[8,64,1024]{2,1,0:T(8,128)(2,1)S(1)}, u32[]{:S(2)}, u32[]{:S(2)}) %all-to-all-start.2) | async-done | bytes 1048608 | tf_op jit(solution)/shard_map/all_to_all | solution.py:188
  264.7 10.5 %all-to-all-start.5 = ((bf16[16,64,128]{2,1,0:T(8,128)(2,1)}), bf16[16,64,128]{2,1,0:T(8,128)(2,1)S(1)}, u32[]{:S(2)}, u32[]{:S(2)}) async-start(bf16[16,64,128]{2,1,0:T(8,128)(2,1)} %bitcast.38), calls=%async_computation.5 | async-start | bytes 524288 | tf_op jit(solution)/shard_map/all_to_all | solution.py:283
  277.1 5.2 %all-to-all-done.5 = bf16[16,64,128]{2,1,0:T(8,128)(2,1)S(1)} async-done(((bf16[16,64,128]{2,1,0:T(8,128)(2,1)}), bf16[16,64,128]{2,1,0:T(8,128)(2,1)S(1)}, u32[]{:S(2)}, u32[]{:S(2)}) %all-to-all-start.5) | async-done | bytes 262176 | tf_op jit(solution)/shard_map/all_to_all | solution.py:283
  282.3 4.2 %all-to-all-start.3 = ((bf16[16,256,128]{2,1,0:T(8,128)(2,1)}), bf16[16,256,128]{2,1,0:T(8,128)(2,1)S(1)}, u32[]{:S(2)}, u32[]{:S(2)}) async-start(bf16[16,256,128]{2,1,0:T(8,128)(2,1)} %bitcast.31), calls=%async_computation.3 | async-start | bytes 2097152 | tf_op jit(solution)/shard_map/all_to_all | solution.py:283
  291.2 2.4 convolution_bitcast_fusion
  296.9 2.5 fusion.9
  303.7 4.2 %fusion.19 = f32[128,448]{0,1:T(8,128)} fusion(f32[128,448]{0,1:T(8,128)S(1)} %copy-done.4, bf16[16,256,128]{2,1,0:T(8,128)(2,1)S(1)} %all-to-all-done.3, bf16[16,320,448]{2,1,0:T(8,128)(2,1)} %bitcast.139), kind=kOutput, calls=%fused_computation.19 | convolution fusion | flops 469819392 | bytes 5701632 | tf_op jit(solution)/shard_map/dot_general | solution.py:285
  (103 shorter events, 34.5 us)
Async XLA Ops:
  7.2 128.3 %copy-start = (bf16[1024,512]{1,0:T(8,128)(2,1)S(1)}, bf16[1024,512]{1,0:T(8,128)(2,1)}, u32[]{:S(2)}) copy-start(bf16[1024,512]{1,0:T(8,128)(2,1)} %param.11) | copy-start | bytes 3145732
  7.2 59.4 %all-gather.4.cloned.1.call-start = ((), (), s32[]{:S(2)}) async-start(), calls=%async_computation.6 | async-start | bytes 6406144 | tf_op jit(solution)/shard_map/all_gather | solution.py:232
  73.9 6.7 %copy-start.3 = (s32[2048]{0:T(1024)S(1)}, s32[2048]{0:T(1024)}, u32[]{:S(2)}) copy-start(s32[2048]{0:T(1024)} %param.9) | copy-start | bytes 24580
  73.9 51.3 %all-to-all-start = ((f32[8,56,2048]{2,1,0:T(8,128)}), f32[8,56,2048]{2,1,0:T(8,128)}, u32[]{:S(2)}, u32[]{:S(2)}) async-start(f32[8,56,2048]{2,1,0:T(8,128)} %pad_maximum_fusion), calls=%async_computation | async-start | bytes 7340032 | tf_op jit(solution)/shard_map/all_to_all | solution.py:227
  79.7 211.5 %all-gather.6.cloned.1.call-start = ((), (), s32[]{:S(2)}) async-start(), calls=%async_computation.7 | async-start | bytes 5570560 | tf_op jit(solution)/shard_map/all_gather | solution.py:298
  127.6 14.5 %collective-permute-start = (bf16[56,2048]{1,0:T(8,128)(2,1)S(1)}, bf16[56,2048]{1,0:T(8,128)(2,1)S(1)}, u32[]{:S(2)}, u32[]{:S(2)}) collective-permute-start(bf16[56,2048]{1,0:T(8,128)(2,1)S(1)} %reduce_sum.55), channel_id=1, source_target_pairs={{0,1},{1,0},{2,3},{3,2},{4,5},{5,4},{6,7},{7,6},{8,9},{9,8},{10,11... | collective-permute-start | bytes 688136 | tf_op jit(solution)/shard_map/ppermute | solution.py:221
  142.3 59.2 %all-to-all-start.1 = ((f32[8,64,2048]{2,1,0:T(8,128)}), f32[8,64,2048]{2,1,0:T(8,128)}, u32[]{:S(2)}, u32[]{:S(2)}) async-start(f32[8,64,2048]{2,1,0:T(8,128)} %bitcast.100), calls=%async_computation.1 | async-start | bytes 8388608 | tf_op jit(solution)/shard_map/all_to_all | solution.py:227
  151.9 24.1 %copy-start.1 = (bf16[15,2048]{1,0:T(8,128)(2,1)}, bf16[15,2048]{1,0:T(8,128)(2,1)S(1)}, u32[]{:S(2)}) copy-start(bf16[15,2048]{1,0:T(8,128)(2,1)S(1)} %broadcast.71) | copy-start | bytes 184324
  176.6 33.0 %collective-permute-start.4 = (f32[16,1024]{1,0:T(8,128)S(1)}, f32[16,1024]{1,0:T(8,128)S(1)}, u32[]{:S(2)}, u32[]{:S(2)}) collective-permute-start(f32[16,1024]{1,0:T(8,128)S(1)} %bitcast.135), channel_id=1, source_target_pairs={{0,1},{1,0},{2,3},{3,2},{4,5},{5,4},{6,7},{7,6},{8,9},{9,8},{10,11... | collective-permute-start | bytes 196616 | tf_op jit(solution)/shard_map/ppermute | solution.py:266
  204.0 16.1 %copy-start.2 = (bf16[15,2048]{1,0:T(8,128)(2,1)S(1)}, bf16[15,2048]{1,0:T(8,128)(2,1)}, u32[]{:S(2)}) copy-start(bf16[15,2048]{1,0:T(8,128)(2,1)} %copy-done.1) | copy-start | bytes 184324
  204.0 14.4 %collective-permute-start.1 = (bf16[64,2048]{1,0:T(8,128)(2,1)S(1)}, bf16[64,2048]{1,0:T(8,128)(2,1)S(1)}, u32[]{:S(2)}, u32[]{:S(2)}) collective-permute-start(bf16[64,2048]{1,0:T(8,128)(2,1)S(1)} %reduce_sum.56), channel_id=1, source_target_pairs={{0,1},{1,0},{2,3},{3,2},{4,5},{5,4},{6,7},{7,6},{8,9},{9,8},{10,11... | collective-permute-start | bytes 786440 | tf_op jit(solution)/shard_map/ppermute | solution.py:221
  210.4 34.6 %all-to-all-start.4 = ((bf16[8,16,1024]{2,1,0:T(8,128)(2,1)}), bf16[8,16,1024]{2,1,0:T(8,128)(2,1)S(1)}, u32[]{:S(2)}, u32[]{:S(2)}) async-start(bf16[8,16,1024]{2,1,0:T(8,128)(2,1)} %broadcast_in_dim.21), calls=%async_computation.4 | async-start | bytes 524288 | tf_op jit(solution)/shard_map/all_to_all | solution.py:188
  235.2 4.2 %collective-permute-start.3 = (f32[]{:T(128)}, f32[]{:T(128)}, u32[]{:S(2)}, u32[]{:S(2)}) collective-permute-start(f32[]{:T(128)} %add.63), channel_id=1, source_target_pairs={{0,1},{1,0},{2,3},{3,2},{4,5},{5,4},{6,7},{7,6},{8,9},{9,8},{10,11... | collective-permute-start | bytes 20 | tf_op jit(solution)/shard_map/ppermute | solution.py:315
  239.3 5.6 %collective-permute-start.2 = (f32[56,1024]{1,0:T(8,128)S(1)}, f32[56,1024]{1,0:T(8,128)S(1)}, u32[]{:S(2)}, u32[]{:S(2)}) collective-permute-start(f32[56,1024]{1,0:T(8,128)S(1)} %bitcast.127), channel_id=1, source_target_pairs={{0,1},{1,0},{2,3},{3,2},{4,5},{5,4},{6,7},{7,6},{8,9},{9,8},{10,11... | collective-permute-start | bytes 688136 | tf_op jit(solution)/shard_map/ppermute | solution.py:266
  246.1 18.6 %all-to-all-start.2 = ((bf16[8,64,1024]{2,1,0:T(8,128)(2,1)}), bf16[8,64,1024]{2,1,0:T(8,128)(2,1)S(1)}, u32[]{:S(2)}, u32[]{:S(2)}) async-start(bf16[8,64,1024]{2,1,0:T(8,128)(2,1)} %broadcast_in_dim.20), calls=%async_computation.2 | async-start | bytes 2097152 | tf_op jit(solution)/shard_map/all_to_all | solution.py:188
  264.7 17.7 %all-to-all-start.5 = ((bf16[16,64,128]{2,1,0:T(8,128)(2,1)}), bf16[16,64,128]{2,1,0:T(8,128)(2,1)S(1)}, u32[]{:S(2)}, u32[]{:S(2)}) async-start(bf16[16,64,128]{2,1,0:T(8,128)(2,1)} %bitcast.38), calls=%async_computation.5 | async-start | bytes 524288 | tf_op jit(solution)/shard_map/all_to_all | solution.py:283
  282.3 20.0 %all-to-all-start.3 = ((bf16[16,256,128]{2,1,0:T(8,128)(2,1)}), bf16[16,256,128]{2,1,0:T(8,128)(2,1)S(1)}, u32[]{:S(2)}, u32[]{:S(2)}) async-start(bf16[16,256,128]{2,1,0:T(8,128)(2,1)} %bitcast.31), calls=%async_computation.3 | async-start | bytes 2097152 | tf_op jit(solution)/shard_map/all_to_all | solution.py:283
  295.6 8.1 %copy-start.4 = (f32[128,448]{0,1:T(8,128)S(1)}, f32[128,448]{0,1:T(8,128)}, u32[]{:S(2)}) copy-start(f32[128,448]{0,1:T(8,128)} %convolution_bitcast_fusion) | copy-start | bytes 688132
Sparse Core Ops, SparseCore 0:
  10.2 56.2 all-gather.3
  82.8 66.2 all-gather.5

commit v4 on v3

--- a/solution.py
+++ b/solution.py
@@ -154,6 +154,94 @@
     )(count, half, *town, *sown, *tall, *sall)
 
 
+def gather_kernel(x_ref, o_ref, here, send, recv):
+    zl, y, c = (lax.axis_index(a) for a in HEAD)
+    ny = lax.axis_size(HEAD[1])
+    size = x_ref.shape[0]
+    low, high = pl.ds(0, size // 2), pl.ds(size // 2, size // 2)
+    up, down, far = lax.rem(y + 1, ny), lax.rem(y + ny - 1, ny), lax.rem(y + 2, ny)
+    sibling, across = {HEAD[2]: 1 - c}, {HEAD[0]: 1 - zl}
+    above, below = {HEAD[1]: up}, {HEAD[1]: down}
+    slot = lambda z, at: (z * ny + at) * 2 + c
+    barrier = pltpu.get_barrier_semaphore()
+    for device in (sibling, across, above, below):
+        pl.semaphore_signal(
+            barrier, inc=1, device_id=device, device_id_type=pl.DeviceIdType.MESH
+        )
+    pl.semaphore_wait(barrier, 4)
+    copies = []
+
+    def push(source, target, device):
+        k = len(copies)
+        copy = pltpu.make_async_remote_copy(
+            src_ref=source,
+            dst_ref=target,
+            send_sem=send.at[k],
+            recv_sem=recv.at[k],
+            device_id=device,
+            device_id_type=pl.DeviceIdType.MESH,
+        )
+        copy.start()
+        copies.append(copy)
+        return copy
+
+    def forward(index, device, part=None):
+        place = o_ref.at[index] if part is None else o_ref.at[index, part]
+        return push(place, place, device)
+
+    own = o_ref.at[slot(zl, y)]
+    first = push(x_ref, own, across)
+    from_down = push(x_ref, own, above)
+    from_up = push(x_ref, own, below)
+    last = [push(x_ref, own, sibling)]
+    keep = pltpu.make_async_copy(x_ref, own, here)
+    keep.start()
+    first.wait_recv()
+    z = 1 - zl
+    cross_down = forward(slot(z, y), above)
+    cross_up = forward(slot(z, y), below)
+    last.append(forward(slot(z, y), sibling))
+    halves = []
+    for plane, lower, upper in ((zl, from_down, from_up), (z, cross_down, cross_up)):
+        lower.wait_recv()
+        half_a = forward(slot(plane, down), above, low)
+        last.append(forward(slot(plane, down), sibling))
+        upper.wait_recv()
+        half_b = forward(slot(plane, up), below, high)
+        last.append(forward(slot(plane, up), sibling))
+        halves.append((plane, half_a, half_b))
+    for plane, half_a, half_b in halves:
+        half_a.wait_recv()
+        half_b.wait_recv()
+        last.append(forward(slot(plane, far), sibling))
+    for copy in last:
+        copy.wait_recv()
+    for copy in copies:
+        copy.wait_send()
+    keep.wait()
+
+
+def gathered(x, collective_id):
+    count = lax.axis_size(HEAD)
+    return pl.pallas_call(
+        gather_kernel,
+        out_shape=jax.ShapeDtypeStruct((count, *x.shape), x.dtype),
+        in_specs=[pl.BlockSpec(memory_space=pltpu.VMEM)],
+        out_specs=pl.BlockSpec(memory_space=pltpu.VMEM),
+        scratch_shapes=[
+            pltpu.SemaphoreType.DMA,
+            pltpu.SemaphoreType.DMA((17,)),
+            pltpu.SemaphoreType.DMA((17,)),
+        ],
+        compiler_params=pltpu.CompilerParams(
+            collective_id=collective_id, has_side_effects=True, vmem_limit_bytes=24 * 2**20
+        ),
+        cost_estimate=pl.CostEstimate(
+            flops=10_000_000_000, bytes_accessed=count * x.size * 2, transcendentals=0
+        ),
+    )(x)
+
+
 def own_tokens(rows, half):
     cut = rows.reshape(rows.shape[0], -1, 2, TILE)
     return lax.dynamic_index_in_dim(cut, half, 2, keepdims=False).reshape(rows.shape[0], -1)
@@ -223,13 +311,12 @@
         high = jnp.where(half == 0, other, own)
         return jnp.concatenate([low, high])
 
-    def reduced(part):
-        arrived = lax.all_to_all(part, ROW, split_axis=0, concat_axis=0, tiled=True)
-        return arrived.sum(axis=0).astype(jnp.bfloat16)
+    def summed(arrived):
+        return swapped(arrived.sum(axis=0).astype(jnp.bfloat16))
 
     for_rows = lambda part: part.reshape(rows, -1, seq_len)
     both = jnp.concatenate([teacher_hidden, student_hidden], axis=1)
-    feats = lax.all_gather(both, HEAD, axis=0, tiled=True)
+    feats = gathered(both, 0).reshape(seq_len, -1)
     teacher_feats = feats[:, : teacher_hidden.shape[1]]
     student_feats = feats[:, teacher_hidden.shape[1] :]
     first = jnp.concatenate(
@@ -239,15 +326,24 @@
         ],
         axis=1,
     )
-    first_rows = swapped(reduced(first))
+    first_rows = summed(lax.all_to_all(first, ROW, split_axis=0, concat_axis=0, tiled=True))
     cut = first_rows.reshape(2, -1, seq_len)
     student_rows = cut[:, : local_heads * s_pad // rows].reshape(-1, seq_len)
     teacher_kv_rows = cut[:, local_heads * s_pad // rows :].reshape(-1, seq_len)
     second = for_rows(project(teacher_query, teacher_feats))
-    second, student_rows, teacher_kv_rows = lax.optimization_barrier(
-        (second, student_rows, teacher_kv_rows)
-    )
-    teacher_q_rows = swapped(reduced(second))
+    spread = jnp.concatenate(
+        [
+            columns_of_heads(student_parts[:1], local_heads, q_pad).T,
+            columns_of_heads(student_parts[1:], local_heads, 2 * sk).T,
+        ]
+    )
+    second, student_rows, teacher_kv_rows, spread = lax.optimization_barrier(
+        (second, student_rows, teacher_kv_rows, spread)
+    )
+    all_weight = gathered(spread, 1)
+    arrived = lax.all_to_all(second, ROW, split_axis=0, concat_axis=0, tiled=True)
+    arrived, all_weight = lax.optimization_barrier((arrived, all_weight))
+    teacher_q_rows = summed(arrived)
 
     def relate(tparts, sparts):
         every = lambda parts: [with_mask_row(a, bias) for a in parts]
@@ -289,14 +385,6 @@
             preferred_element_type=jnp.float32,
         )
 
-    spread = jnp.concatenate(
-        [
-            columns_of_heads(student_parts[:1], local_heads, q_pad).T,
-            columns_of_heads(student_parts[1:], local_heads, 2 * sk).T,
-        ]
-    )
-    all_weight = lax.all_gather(spread, HEAD, axis=0, tiled=False)
-
     kv_grad, kv_loss = relate(
         [teacher_kv_rows[:tk], teacher_kv_rows[tk:]],
         [student_rows[sq : sq + sk], student_rows[sq + sk : sq + 2 * sk]],

time: 316 us -> 302 us (0.956)
  Pallas kernels: 37.2 us -> 115 us
  waiting for transfers between devices: 139 us -> 65.8 us
  between operations: 23.1 us -> 9.74 us
  starting transfers between devices: 59.9 us -> 53 us
  local copies, waits for them, and re-layouts: 20.3 us -> 24.7 us
    pallas_call x0 -> x2, Pallas kernels: none -> 78 us  [gathered(): pl.pallas_call(gather_kernel, out_shape=jax.ShapeDtypeStruct((count, *x.s...]
    all_gather x2 -> x0, waiting for transfers between devices: 53.5 us -> none  [the longest x1 53.5 us: per_device(): feats = lax.all_gather(both, HEAD, axis=0, tiled=True)]
    all_to_all x2, waiting for transfers between devices: 67.3 us -> 38.8 us  [the longest x1 38.8 us: per_device(): lax.all_to_all(first, ROW, split_axis=0, concat_axis=0, tiled=True)]
    all_to_all x2, starting transfers between devices: 14.6 us -> 8.31 us  [token_grads(): got = lax.all_to_all(blocks, HEAD, split_axis=0, concat_axis=0, tiled=True)]
    all_to_all x2, waiting for transfers between devices: 11 us -> 15.5 us  [copy_for_each(): lax.all_to_all(jnp.broadcast_to(value[None], (size, *value.shape)), axis,...]
    ppermute x2, waiting for transfers between devices: 0.01 us -> 4.06 us  [swapped(): other = lax.ppermute(own, ROW[1], swap)]
    unnamed x21, local copies, waits for them, and re-layouts: 3.84 us -> 7.15 us
  transfers between devices with their start and end apart: 13 -> 11, of which waited for: 6 -> 5; matrix products, arithmetic and copies ran while one was open for 13% -> 12% of each run, Pallas kernels for 12% -> 27%
where the time goes in v4:
time: 302 us; the launch traced here: 300 us
  Pallas kernels  115 us (38%)
  waiting for transfers between devices  65.8 us (22%)
  starting transfers between devices  53 us (18%)
  local copies, waits for them, and re-layouts  24.7 us (8%)
  matrix products  20.2 us (7%)
  other arithmetic  11.9 us (4%)
  between operations  9.74 us (3%)
    pallas_call x2, Pallas kernels, gathered(): pl.pallas_call(gather_kernel, out_shape=jax.ShapeDtypeStruct((count, *x.s...  78 us
    all_to_all x1, waiting for transfers between devices, per_device(): lax.all_to_all(first, ROW, split_axis=0, concat_axis=0, tiled=True)  38.8 us
    pallas_call x2, Pallas kernels, relations(): pl.pallas_call(functools.partial(relation_kernel, tdims, sdims), grid=(mi...  37.2 us
    all_to_all x2, waiting for transfers between devices, copy_for_each(): lax.all_to_all(jnp.broadcast_to(value[None], (size, *value.shape)), axis,...  15.5 us
    all_to_all x2, starting transfers between devices, copy_for_each(): lax.all_to_all(jnp.broadcast_to(value[None], (size, *value.shape)), axis,...  14.5 us
    ppermute x2, starting transfers between devices, swapped(): other = lax.ppermute(own, ROW[1], swap)  11.3 us
    dot_general x3, matrix products, project(): lax.dot_general(weight, feats, (((0,), (1,)), ((), ())), preferred_elemen...  8.96 us
    all_to_all x2, starting transfers between devices, token_grads(): got = lax.all_to_all(blocks, HEAD, split_axis=0, concat_axis=0, tiled=True)  8.31 us
  transfers between devices with their start and end apart: 11, of which 5 were waited for; matrix products, arithmetic and copies ran while one was open for 12% of the time, Pallas kernels for 27%

profile of v4, /device:TPU:1, one launch (start us, length us, event | category | flops | bytes accessed | tf_op | source)
XLA Modules:
  0.0 300.4 jit_solution(17367148366528649606)
XLA Ops:
  5.6 34.7 %shard_map.102 = bf16[16,128,1472]{2,1,0:T(8,128)(2,1)S(1)} custom-call(bf16[128,1472]{1,0:T(8,128)(2,1)S(1)} %pad_maximum_fusion.4.x_ref), custom_call_target="tpu_custom_call" | custom-call | flops 10000000000 | bytes 6029312 | tf_op jit(solution)/shard_map/pallas_call | solution.py:226
  43.9 2.3 pad_maximum_fusion
  46.1 7.2 %all-to-all-start = ((f32[8,56,2048]{2,1,0:T(8,128)}), f32[8,56,2048]{2,1,0:T(8,128)}, u32[]{:S(2)}, u32[]{:S(2)}) async-start(f32[8,56,2048]{2,1,0:T(8,128)} %pad_maximum_fusion), calls=%async_computation | async-start | bytes 7340032 | tf_op jit(solution)/shard_map/all_to_all | solution.py:329
  53.4 6.6 %fusion.5 = f32[2048,512]{0,1:T(8,128)} fusion(bf16[1024,512]{1,0:T(8,128)(2,1)S(1)} %copy-done, bf16[2048,1472]{1,0:T(8,128)(2,1)} %bitcast.105), kind=kOutput, calls=%fused_computation.5 | convolution fusion | flops 2147483648 | bytes 9437184 | tf_op jit(solution)/shard_map/dot_general | solution.py:304
  60.0 38.8 %all-to-all-done = f32[8,56,2048]{2,1,0:T(8,128)} async-done(((f32[8,56,2048]{2,1,0:T(8,128)}), f32[8,56,2048]{2,1,0:T(8,128)}, u32[]{:S(2)}, u32[]{:S(2)}) %all-to-all-start) | async-done | bytes 3670048 | tf_op jit(solution)/shard_map/all_to_all | solution.py:329
  98.9 2.3 reduce_sum.55
  101.2 7.9 %collective-permute-start = (bf16[56,2048]{1,0:T(8,128)(2,1)S(1)}, bf16[56,2048]{1,0:T(8,128)(2,1)S(1)}, u32[]{:S(2)}, u32[]{:S(2)}) collective-permute-start(bf16[56,2048]{1,0:T(8,128)(2,1)S(1)} %reduce_sum.55), channel_id=1, source_target_pairs={{0,1},{1,0},{2,3},{3,2},{4,5},{5,4},{6,7},{7,6},{8,9},{9,8},{10,11... | collective-permute-start | bytes 688136 | tf_op jit(solution)/shard_map/ppermute | solution.py:309
  109.8 4.1 %collective-permute-done = bf16[56,2048]{1,0:T(8,128)(2,1)S(1)} collective-permute-done((bf16[56,2048]{1,0:T(8,128)(2,1)S(1)}, bf16[56,2048]{1,0:T(8,128)(2,1)S(1)}, u32[]{:S(2)}, u32[]{:S(2)}) %collective-permute-start) | collective-permute-done | bytes 229408 | tf_op jit(solution)/shard_map/ppermute | solution.py:309
  114.0 7.9 %all-to-all-start.1 = ((f32[8,64,2048]{2,1,0:T(8,128)}), f32[8,64,2048]{2,1,0:T(8,128)}, u32[]{:S(2)}, u32[]{:S(2)}) async-start(f32[8,64,2048]{2,1,0:T(8,128)} %bitcast.108), calls=%async_computation.1 | async-start | bytes 8388608 | tf_op jit(solution)/shard_map/all_to_all | solution.py:344
  122.7 24.0 %shard_map.105 = (f32[16,1024]{1,0:T(8,128)S(1)}, f32[16,2048]{1,0:T(8,128)S(1)}, f32[32,128]{1,0:T(8,128)S(1)}) custom-call(s32[1]{0:T(128)} %bitcast.n_ref, s32[1]{0:T(128)} %bitcast.1.p_ref, bf16[32,1024]{1,0:T(8,128)(2,1)S(1)} %get-tuple-element.71.refs_0_, bf16[32,1024]{1,0:T(8,128)(2,1)S(1)} %get-tuple-element.70.refs_1_, ...), custom_call_target="tpu_custom_call" | custom-call | flops 20000000000 | bytes 4194304 | tf_op jit(solution)/shard_map/pallas_call | solution.py:127
  149.8 43.3 %shard_map.103 = bf16[16,320,448]{2,1,0:T(8,128)(2,1)S(1)} custom-call(bf16[320,448]{1,0:T(8,128)(2,1)S(1)} %pad_maximum_fusion.5.x_ref), custom_call_target="tpu_custom_call" | custom-call | flops 10000000000 | bytes 4587520 | tf_op jit(solution)/shard_map/pallas_call | solution.py:226
  193.1 2.4 copy-done.2
  195.5 2.5 reduce_sum.56
  198.0 3.3 %collective-permute-start.1 = (bf16[64,2048]{1,0:T(8,128)(2,1)S(1)}, bf16[64,2048]{1,0:T(8,128)(2,1)S(1)}, u32[]{:S(2)}, u32[]{:S(2)}) collective-permute-start(bf16[64,2048]{1,0:T(8,128)(2,1)S(1)} %reduce_sum.56), channel_id=1, source_target_pairs={{0,1},{1,0},{2,3},{3,2},{4,5},{5,4},{6,7},{7,6},{8,9},{9,8},{10,11... | collective-permute-start | bytes 786440 | tf_op jit(solution)/shard_map/ppermute | solution.py:309
  202.7 7.8 %all-to-all-start.4 = ((bf16[8,16,1024]{2,1,0:T(8,128)(2,1)}), bf16[8,16,1024]{2,1,0:T(8,128)(2,1)}, u32[]{:S(2)}, u32[]{:S(2)}) async-start(bf16[8,16,1024]{2,1,0:T(8,128)(2,1)} %broadcast_in_dim.21), calls=%async_computation.4 | async-start | bytes 524288 | tf_op jit(solution)/shard_map/all_to_all | solution.py:276
  212.3 13.2 %shard_map.104 = (f32[56,1024]{1,0:T(8,128)S(1)}, f32[56,2048]{1,0:T(8,128)S(1)}, f32[32,128]{1,0:T(8,128)S(1)}) custom-call(s32[1]{0:T(128)} %bitcast.n_ref, s32[1]{0:T(128)} %bitcast.1.p_ref, bf16[144,1024]{1,0:T(8,128)(2,1)S(1)} %pad_maximum_fusion.6.refs_0_, bf16[64,1024]{1,0:T(8,128)(2,1)S(1)} %pad_maximum_fusion.13.refs_1_, ...), custom_call_target="tpu_custom_call" | custom-call | flops 10000000000 | bytes 4194304 | tf_op jit(solution)/shard_map/pallas_call | solution.py:127
  238.3 6.6 %all-to-all-start.2 = ((bf16[8,64,1024]{2,1,0:T(8,128)(2,1)}), bf16[8,64,1024]{2,1,0:T(8,128)(2,1)S(1)}, u32[]{:S(2)}, u32[]{:S(2)}) async-start(bf16[8,64,1024]{2,1,0:T(8,128)(2,1)} %broadcast_in_dim.20), calls=%async_computation.2 | async-start | bytes 2097152 | tf_op jit(solution)/shard_map/all_to_all | solution.py:276
  246.8 15.5 %all-to-all-done.2 = bf16[8,64,1024]{2,1,0:T(8,128)(2,1)S(1)} async-done(((bf16[8,64,1024]{2,1,0:T(8,128)(2,1)}), bf16[8,64,1024]{2,1,0:T(8,128)(2,1)S(1)}, u32[]{:S(2)}, u32[]{:S(2)}) %all-to-all-start.2) | async-done | bytes 1048608 | tf_op jit(solution)/shard_map/all_to_all | solution.py:276
  262.3 4.1 %all-to-all-start.5 = ((bf16[16,64,128]{2,1,0:T(8,128)(2,1)}), bf16[16,64,128]{2,1,0:T(8,128)(2,1)S(1)}, u32[]{:S(2)}, u32[]{:S(2)}) async-start(bf16[16,64,128]{2,1,0:T(8,128)(2,1)} %bitcast.43), calls=%async_computation.5 | async-start | bytes 524288 | tf_op jit(solution)/shard_map/all_to_all | solution.py:379
  268.4 5.3 %all-to-all-done.5 = bf16[16,64,128]{2,1,0:T(8,128)(2,1)S(1)} async-done(((bf16[16,64,128]{2,1,0:T(8,128)(2,1)}), bf16[16,64,128]{2,1,0:T(8,128)(2,1)S(1)}, u32[]{:S(2)}, u32[]{:S(2)}) %all-to-all-start.5) | async-done | bytes 262176 | tf_op jit(solution)/shard_map/all_to_all | solution.py:379
  273.7 4.2 %all-to-all-start.3 = ((bf16[16,256,128]{2,1,0:T(8,128)(2,1)}), bf16[16,256,128]{2,1,0:T(8,128)(2,1)S(1)}, u32[]{:S(2)}, u32[]{:S(2)}) async-start(bf16[16,256,128]{2,1,0:T(8,128)(2,1)} %bitcast.36), calls=%async_computation.3 | async-start | bytes 2097152 | tf_op jit(solution)/shard_map/all_to_all | solution.py:379
  282.5 2.4 convolution_bitcast_fusion
  288.2 2.5 fusion.9
  295.1 4.2 %fusion.19 = f32[128,448]{0,1:T(8,128)} fusion(f32[128,448]{0,1:T(8,128)S(1)} %copy-done.4, bf16[16,256,128]{2,1,0:T(8,128)(2,1)S(1)} %all-to-all-done.3, bf16[16,320,448]{2,1,0:T(8,128)(2,1)} %copy-done.2), kind=kOutput, calls=%fused_computation.19 | convolution fusion | flops 469819392 | bytes 5701632 | tf_op jit(solution)/shard_map/dot_general | solution.py:381
  (99 shorter events, 37.4 us)
Async XLA Ops:
  0.6 52.8 %copy-start = (bf16[1024,512]{1,0:T(8,128)(2,1)S(1)}, bf16[1024,512]{1,0:T(8,128)(2,1)}, u32[]{:S(2)}) copy-start(bf16[1024,512]{1,0:T(8,128)(2,1)} %param.11) | copy-start | bytes 3145732
  40.3 2.7 copy-start.1
  46.1 7.2 %copy-start.3 = (s32[2048]{0:T(1024)S(1)}, s32[2048]{0:T(1024)}, u32[]{:S(2)}) copy-start(s32[2048]{0:T(1024)} %param.9) | copy-start | bytes 24580
  46.1 52.7 %all-to-all-start = ((f32[8,56,2048]{2,1,0:T(8,128)}), f32[8,56,2048]{2,1,0:T(8,128)}, u32[]{:S(2)}, u32[]{:S(2)}) async-start(f32[8,56,2048]{2,1,0:T(8,128)} %pad_maximum_fusion), calls=%async_computation | async-start | bytes 7340032 | tf_op jit(solution)/shard_map/all_to_all | solution.py:329
  101.2 12.7 %collective-permute-start = (bf16[56,2048]{1,0:T(8,128)(2,1)S(1)}, bf16[56,2048]{1,0:T(8,128)(2,1)S(1)}, u32[]{:S(2)}, u32[]{:S(2)}) collective-permute-start(bf16[56,2048]{1,0:T(8,128)(2,1)S(1)} %reduce_sum.55), channel_id=1, source_target_pairs={{0,1},{1,0},{2,3},{3,2},{4,5},{5,4},{6,7},{7,6},{8,9},{9,8},{10,11... | collective-permute-start | bytes 688136 | tf_op jit(solution)/shard_map/ppermute | solution.py:309
  114.0 81.5 %all-to-all-start.1 = ((f32[8,64,2048]{2,1,0:T(8,128)}), f32[8,64,2048]{2,1,0:T(8,128)}, u32[]{:S(2)}, u32[]{:S(2)}) async-start(f32[8,64,2048]{2,1,0:T(8,128)} %bitcast.108), calls=%async_computation.1 | async-start | bytes 8388608 | tf_op jit(solution)/shard_map/all_to_all | solution.py:344
  147.3 54.6 %collective-permute-start.4 = (f32[16,1024]{1,0:T(8,128)S(1)}, f32[16,1024]{1,0:T(8,128)S(1)}, u32[]{:S(2)}, u32[]{:S(2)}) collective-permute-start(f32[16,1024]{1,0:T(8,128)S(1)} %bitcast.143), channel_id=1, source_target_pairs={{0,1},{1,0},{2,3},{3,2},{4,5},{5,4},{6,7},{7,6},{8,9},{9,8},{10,11... | collective-permute-start | bytes 196616 | tf_op jit(solution)/shard_map/ppermute | solution.py:362
  193.1 2.4 copy-start.2
  198.0 12.5 %collective-permute-start.1 = (bf16[64,2048]{1,0:T(8,128)(2,1)S(1)}, bf16[64,2048]{1,0:T(8,128)(2,1)S(1)}, u32[]{:S(2)}, u32[]{:S(2)}) collective-permute-start(bf16[64,2048]{1,0:T(8,128)(2,1)S(1)} %reduce_sum.56), channel_id=1, source_target_pairs={{0,1},{1,0},{2,3},{3,2},{4,5},{5,4},{6,7},{7,6},{8,9},{9,8},{10,11... | collective-permute-start | bytes 786440 | tf_op jit(solution)/shard_map/ppermute | solution.py:309
  202.7 34.5 %all-to-all-start.4 = ((bf16[8,16,1024]{2,1,0:T(8,128)(2,1)}), bf16[8,16,1024]{2,1,0:T(8,128)(2,1)}, u32[]{:S(2)}, u32[]{:S(2)}) async-start(bf16[8,16,1024]{2,1,0:T(8,128)(2,1)} %broadcast_in_dim.21), calls=%async_computation.4 | async-start | bytes 524288 | tf_op jit(solution)/shard_map/all_to_all | solution.py:276
  227.4 4.2 %collective-permute-start.3 = (f32[]{:T(128)}, f32[]{:T(128)}, u32[]{:S(2)}, u32[]{:S(2)}) collective-permute-start(f32[]{:T(128)} %add.63), channel_id=1, source_target_pairs={{0,1},{1,0},{2,3},{3,2},{4,5},{5,4},{6,7},{7,6},{8,9},{9,8},{10,11... | collective-permute-start | bytes 20 | tf_op jit(solution)/shard_map/ppermute | solution.py:403
  231.5 5.6 %collective-permute-start.2 = (f32[56,1024]{1,0:T(8,128)S(1)}, f32[56,1024]{1,0:T(8,128)S(1)}, u32[]{:S(2)}, u32[]{:S(2)}) collective-permute-start(f32[56,1024]{1,0:T(8,128)S(1)} %bitcast.135), channel_id=1, source_target_pairs={{0,1},{1,0},{2,3},{3,2},{4,5},{5,4},{6,7},{7,6},{8,9},{9,8},{10,11... | collective-permute-start | bytes 688136 | tf_op jit(solution)/shard_map/ppermute | solution.py:362
  238.3 24.0 %all-to-all-start.2 = ((bf16[8,64,1024]{2,1,0:T(8,128)(2,1)}), bf16[8,64,1024]{2,1,0:T(8,128)(2,1)S(1)}, u32[]{:S(2)}, u32[]{:S(2)}) async-start(bf16[8,64,1024]{2,1,0:T(8,128)(2,1)} %broadcast_in_dim.20), calls=%async_computation.2 | async-start | bytes 2097152 | tf_op jit(solution)/shard_map/all_to_all | solution.py:276
  262.3 11.4 %all-to-all-start.5 = ((bf16[16,64,128]{2,1,0:T(8,128)(2,1)}), bf16[16,64,128]{2,1,0:T(8,128)(2,1)S(1)}, u32[]{:S(2)}, u32[]{:S(2)}) async-start(bf16[16,64,128]{2,1,0:T(8,128)(2,1)} %bitcast.43), calls=%async_computation.5 | async-start | bytes 524288 | tf_op jit(solution)/shard_map/all_to_all | solution.py:379
  273.7 20.1 %all-to-all-start.3 = ((bf16[16,256,128]{2,1,0:T(8,128)(2,1)}), bf16[16,256,128]{2,1,0:T(8,128)(2,1)S(1)}, u32[]{:S(2)}, u32[]{:S(2)}) async-start(bf16[16,256,128]{2,1,0:T(8,128)(2,1)} %bitcast.36), calls=%async_computation.3 | async-start | bytes 2097152 | tf_op jit(solution)/shard_map/all_to_all | solution.py:379
  288.2 6.9 %copy-start.4 = (f32[128,448]{0,1:T(8,128)S(1)}, f32[128,448]{0,1:T(8,128)}, u32[]{:S(2)}) copy-start(f32[128,448]{0,1:T(8,128)} %convolution_bitcast_fusion) | copy-start | bytes 688132
